TPU v7x, 256 devices: a whole 4x4x8 slice. The times are simulated.
256 devices in a mesh: lon: 16 (over z, y_hi), lat: 8 (over x, core), mem: 2 (over y_lo).
Axes of the slice: x: 4, y: 4 (y_hi: 2, y_lo: 2; y = y_hi * 2 + y_lo), z: 8, core: 2. Of those that a mesh axis runs over, the one named last changes fastest.
Arguments:
- tokens: bfloat16 [4, 8, 272, 96, 192], P('mem', None, 'lat', 'lon'), parts along dimension 0, may hold values from -6 to 6
- band_rows: int32 [8, 2], P('lat'), may hold values from 0 to 177, as said below
- down_gain: float32 [768], replicated, may hold values from 0.1 to 1.9
- down_shift: float32 [768], replicated, may hold values from -3 to 3
- down_weight: bfloat16 [768, 384], P(('lon', 'lat')), may hold values from -0.21875 to 0.21875
- up_weight: bfloat16 [384, 768], P(('lon', 'lat')), may hold values from -0.3125 to 0.3125
- up_gain: float32 [192], replicated, may hold values from 0.1 to 1.9
- up_shift: float32 [192], replicated, may hold values from -3 to 3
- mix_weight: bfloat16 [192, 192], replicated, may hold values from -0.4375 to 0.4375
Outputs:
- expanded: bfloat16 [4, 8, 272, 96, 192], P('mem', None, 'lat', 'lon'), parts along dimension 0
There are 2 independent parts, one for each index of `mem`. A program takes and returns all parts, laid end to end along the dimension named above; an argument that names none is the same for every part. Nothing has to cross between parts.
Inputs may be any that keep to these rules, and one draw needn't show every extreme that they name: `band_rows`: row b holds band b's first latitude row and one past its last; the bands cover rows 0 to 176 in order without gaps; band 0 holds an odd number of rows and every other band an even number; each band holds at least 2 * (5) rows and at most 34, and some band other than band 0 holds exactly 34.
All inputs are finite; a program needn't handle non-finite values.
Results may differ from a plain program's by a relative error of at most 0.0062.
Values may be sent and summed in bfloat16 or wider, within the bound.
A program may use at most 64 MiB of HBM per device.

v0:
```python
import jax
import jax.numpy as jnp
from jax import lax
from jax.sharding import PartitionSpec as P


def shifted(block, axis, distance):
    devices = range(lax.axis_size(axis))
    route = [((i - distance) % len(devices), i) for i in devices]
    return lax.ppermute(block, axis, route)


def passed_along(block, axis, distance):
    devices = range(lax.axis_size(axis))
    route = [(i - distance, i) for i in devices if i - distance in devices]
    return lax.ppermute(block, axis, route)


def in_order(tiles, dim):
    shape = list(tiles.shape[1:])
    shape[dim] *= tiles.shape[0]
    return jnp.moveaxis(tiles, 0, dim).reshape(shape)


def from_everyone(x, axis):
    copies = jnp.broadcast_to(x, (lax.axis_size(axis), *x.shape))
    return lax.all_to_all(copies, axis, split_axis=0, concat_axis=0, tiled=True)


def gather_directly(x, axis, dim):
    return in_order(from_everyone(x, axis), dim)


def normalize(values, scale_gain, bias_shift):
    average = jnp.mean(values, axis=-1, keepdims=True)
    centred = values - average
    spread = jnp.mean(centred * centred, axis=-1, keepdims=True)
    return centred * lax.rsqrt(spread + 1e-05) * scale_gain + bias_shift


def body(
    tokens, band_rows, down_gain, down_shift, down_weight, up_weight, up_gain, up_shift, mix_weight
):
    members, levels, slot_count, columns, features = tokens.shape
    half_rows = slot_count // 2 + 1
    first_row = band_rows[0, 0]
    live_rows = band_rows[0, 1] - first_row
    lat_odd = first_row % 2
    row_ids = lax.broadcasted_iota(jnp.int32, (1, 1, slot_count, 1, 1), 2)
    fields = jnp.where(row_ids < live_rows, tokens, jnp.zeros_like(tokens))
    right_col = shifted(fields[:, :, :, :1], "lon", -1)
    window = jnp.concatenate([fields[:, :, :, 1:], right_col], axis=3)
    window_cols = window.shape[3]
    half_cols = window_cols // 2
    next_first = passed_along(window[:, :, :1], "lat", -1)
    zero_rows = jnp.zeros((members, levels, 2, window_cols, features), window.dtype)
    extended = jnp.concatenate([window, zero_rows, zero_rows[:, :, :1]], axis=2)
    ext_ids = lax.broadcasted_iota(jnp.int32, (1, 1, slot_count + 3, 1, 1), 2)
    extended = jnp.where(ext_ids == live_rows, next_first, extended)
    patch_rows = lax.dynamic_slice_in_dim(extended, lat_odd, 2 * half_rows, 2)
    merged = patch_rows.reshape(members, levels, half_rows, 2, half_cols, 2, features)
    merged = merged.transpose(0, 1, 2, 4, 5, 3, 6).reshape(
        members * levels * half_rows * half_cols, 4 * features
    )
    merged_norm = normalize(merged.astype(jnp.float32), down_gain, down_shift).astype(jnp.bfloat16)
    band_down = gather_directly(down_weight, "lat", 0)
    columns_used = merged_norm
    coarse = jnp.dot(
        columns_used, gather_directly(band_down, "lon", 0), preferred_element_type=jnp.float32
    )
    coarse = coarse.astype(jnp.bfloat16)
    band_up = gather_directly(up_weight, "lat", 0)
    columns_used = coarse
    grown = jnp.dot(
        columns_used, gather_directly(band_up, "lon", 0), preferred_element_type=jnp.float32
    )
    grown = grown.reshape(members, levels, half_rows, half_cols, 2, 2, features)
    grown = grown.transpose(0, 1, 2, 4, 3, 5, 6).reshape(
        members, levels, 2 * half_rows, window_cols, features
    )
    fine_norm = normalize(grown, up_gain, up_shift).astype(jnp.bfloat16)
    fine_out = jnp.dot(
        fine_norm.reshape(-1, features), mix_weight, preferred_element_type=jnp.float32
    )
    fine_out = fine_out.astype(jnp.bfloat16).reshape(
        members, levels, 2 * half_rows, window_cols, features
    )
    overflow_row = lax.dynamic_slice_in_dim(fine_out, live_rows - lat_odd, 1, 2)
    from_above = passed_along(overflow_row, "lat", 1)
    padded_rows = jnp.concatenate([jnp.zeros_like(overflow_row), fine_out], axis=2)
    owned = lax.dynamic_slice_in_dim(padded_rows, 1 - lat_odd, slot_count, 2)
    owned = jnp.where((row_ids == 0) & (lat_odd == 1), from_above, owned)
    overflow_col = owned[:, :, :, columns - 1 :]
    from_left = shifted(overflow_col, "lon", 1)
    owned = jnp.concatenate([from_left, owned[:, :, :, : columns - 1]], axis=3)
    return jnp.where(row_ids < live_rows, owned, jnp.zeros_like(owned))


def solution(mesh):
    return jax.shard_map(
        body,
        mesh=mesh,
        in_specs=(
            P("mem", None, "lat", "lon", None),
            P("lat", None),
            P(),
            P(),
            P(("lon", "lat"), None),
            P(("lon", "lat"), None),
            P(),
            P(),
            P(),
        ),
        out_specs=P("mem", None, "lat", "lon", None),
        check_vma=False,
    )
```

profile of v0, /device:TPU:1, one launch (start us, length us, event | category | flops | bytes accessed | tf_op | source)
XLA Modules:
  0.0 141.1 jit_solution(8208039982380259431)
XLA Ops:
  0.0 1.3 broadcast_in_dim.76
  1.4 6.4 %all-to-all-start = ((bf16[8,6,384]{2,1,0:T(8,128)(2,1)}), bf16[8,6,384]{2,1,0:T(8,128)(2,1)S(1)}, u32[]{:S(2)}, u32[]{:S(2)}) async-start(bf16[8,6,384]{2,1,0:T(8,128)(2,1)} %broadcast_in_dim.76), calls=%async_computation | async-start | bytes 98304 | tf_op jit(solution)/shard_map/all_to_all | solution.py:27
  7.8 1.3 fusion.20
  10.3 2.3 %all-to-all-done = bf16[8,6,384]{2,1,0:T(8,128)(2,1)S(1)} async-done(((bf16[8,6,384]{2,1,0:T(8,128)(2,1)}), bf16[8,6,384]{2,1,0:T(8,128)(2,1)S(1)}, u32[]{:S(2)}, u32[]{:S(2)}) %all-to-all-start) | async-done | bytes 36896 | tf_op jit(solution)/shard_map/all_to_all | solution.py:27
  12.6 1.3 broadcast_in_dim.78
  13.9 4.0 %all-to-all-start.2 = ((bf16[8,3,768]{2,1,0:T(4,128)(2,1)}), bf16[8,3,768]{2,1,0:T(4,128)(2,1)S(1)}, u32[]{:S(2)}, u32[]{:S(2)}) async-start(bf16[8,3,768]{2,1,0:T(4,128)(2,1)} %broadcast_in_dim.78), calls=%async_computation.2 | async-start | bytes 98304 | tf_op jit(solution)/shard_map/all_to_all | solution.py:27
  18.0 4.8 %all-to-all-done.2 = bf16[8,3,768]{2,1,0:T(4,128)(2,1)S(1)} async-done(((bf16[8,3,768]{2,1,0:T(4,128)(2,1)}), bf16[8,3,768]{2,1,0:T(4,128)(2,1)S(1)}, u32[]{:S(2)}, u32[]{:S(2)}) %all-to-all-start.2) | async-done | bytes 36896 | tf_op jit(solution)/shard_map/all_to_all | solution.py:27
  22.7 0.9 broadcast_in_dim.77
  23.6 10.3 %all-to-all-start.1 = ((bf16[16,48,384]{2,1,0:T(8,128)(2,1)}), bf16[16,48,384]{2,1,0:T(8,128)(2,1)}, u32[]{:S(2)}, u32[]{:S(2)}) async-start(bf16[16,48,384]{2,1,0:T(8,128)(2,1)} %broadcast_in_dim.77), calls=%async_computation.1 | async-start | bytes 1179648 | tf_op jit(solution)/shard_map/all_to_all | solution.py:27
  33.9 1.6 %broadcast_select_fusion = bf16[2,8,34,6,192]{4,1,3,2,0:T(8,128)(2,1)S(1)} fusion(bf16[2,8,34,6,192]{4,1,3,2,0:T(8,128)(2,1)} %param.9, pred[34]{0:T(512)(128)(4,1)S(1)} %iota_compare_fusion.1), kind=kLoop, calls=%fused_computation.26 | loop fusion | flops 626688 | bytes 2506786 | tf_op jit(solution)/shard_map/jit(_where)/select_n | solution.py:50
  35.5 0.7 slice.29
  36.3 4.9 %collective-permute-start = (bf16[2,8,34,1,192]{4,1,3,2,0:T(8,128)(2,1)}, bf16[2,8,34,1,192]{4,1,3,2,0:T(8,128)(2,1)S(1)}, u32[]{:S(2)}, u32[]{:S(2)}) collective-permute-start(bf16[2,8,34,1,192]{4,1,3,2,0:T(8,128)(2,1)} %slice.29), channel_id=1, source_target_pairs={{16,0},{32,16},{48,32},{64,48},{80,64},{96,80},{112,96},{128,112},... | collective-permute-start | bytes 626696 | tf_op jit(solution)/shard_map/ppermute | solution.py:10
  43.1 0.0 copy-start.3
  43.1 0.0 copy-start.4
  43.1 0.1 slice.28
  43.2 8.8 %collective-permute-done = bf16[2,8,34,1,192]{4,1,3,2,0:T(8,128)(2,1)S(1)} collective-permute-done((bf16[2,8,34,1,192]{4,1,3,2,0:T(8,128)(2,1)}, bf16[2,8,34,1,192]{4,1,3,2,0:T(8,128)(2,1)S(1)}, u32[]{:S(2)}, u32[]{:S(2)}) %collective-permute-start) | collective-permute-done | bytes 208928 | tf_op jit(solution)/shard_map/ppermute | solution.py:10
  52.1 3.5 %collective-permute-start.1 = (bf16[2,8,1,6,192]{4,1,3,2,0:T(8,128)(2,1)S(1)}, bf16[2,8,1,6,192]{4,1,3,2,0:T(8,128)(2,1)S(1)}, u32[]{:S(2)}, u32[]{:S(2)}) collective-permute-start(bf16[2,8,1,6,192]{4,1,3,2,0:T(8,128)(2,1)S(1)} %pad_maximum_fusion), channel_id=1, source_target_pairs={{2,0},{4,2},{6,4},{8,6},{10,8},{12,10},{14,12},{3,1},{5,3},{7,5},{... | collective-permute-start | bytes 110600 | tf_op jit(solution)/shard_map/ppermute | solution.py:16
  55.6 0.1 pad_dynamic-slice_fusion.3
  55.7 0.6 dynamic-slice.2
  56.3 0.1 pad.6.clone
  56.4 0.6 dynamic-slice.1
  57.0 0.0 copy-done.3
  57.0 0.1 mul.49
  57.1 0.1 add.63
  57.2 0.6 reshape.127
  57.8 0.0 collective-permute-done.1
  57.8 0.6 copy-done.2
  58.5 1.4 fusion.11
  59.9 0.4 fusion.1
  60.3 0.0 all-to-all-done.1
  60.3 0.3 copy-done.1
  60.6 0.9 broadcast_in_dim.79
  61.5 10.8 %all-to-all-start.3 = ((bf16[16,24,768]{2,1,0:T(8,128)(2,1)}), bf16[16,24,768]{2,1,0:T(8,128)(2,1)}, u32[]{:S(2)}, u32[]{:S(2)}) async-start(bf16[16,24,768]{2,1,0:T(8,128)(2,1)} %broadcast_in_dim.79), calls=%async_computation.3 | async-start | bytes 1179648 | tf_op jit(solution)/shard_map/all_to_all | solution.py:27
  72.3 0.7 fusion.4
  73.1 0.7 fusion.7
  73.8 1.4 copy.47
  75.1 1.3 convert_element_type.32
  76.4 1.9 %convolution_convert_fusion.1 = bf16[864,384]{1,0:T(8,128)(2,1)S(1)} fusion(bf16[864,768]{1,0:T(8,128)(2,1)S(1)} %convert_element_type.32, bf16[768,384]{1,0:T(8,128)(2,1)} %bitcast.6), kind=kOutput, calls=%fused_computation.27 | convolution fusion | flops 509939712 | bytes 2580480 | tf_op jit(solution)/shard_map/dot_general | solution.py:68
  78.3 0.3 dot_general.16
  78.7 14.0 %all-to-all-done.3 = bf16[16,24,768]{2,1,0:T(8,128)(2,1)} async-done(((bf16[16,24,768]{2,1,0:T(8,128)(2,1)}), bf16[16,24,768]{2,1,0:T(8,128)(2,1)}, u32[]{:S(2)}, u32[]{:S(2)}) %all-to-all-start.3) | async-done | bytes 589856 | tf_op jit(solution)/shard_map/all_to_all | solution.py:27
  92.7 1.4 copy.48
  94.1 3.6 %fusion.21 = (f32[2,8,18,2,3,2]{2,5,3,4,1,0:T(2,128)S(1)}, f32[2,8,18,2,3,2,192]{6,2,5,3,4,1,0:T(8,128)}) fusion(bf16[2,2,192,384,1,1,1]{3,2,1,0,6,5,4:T(8,128)(2,1)S(1)} %bitcast.49, bf16[2,8,18,3,384,1,1]{4,3,2,1,0,6,5:T(4,128)(2,1)S(1)} %bitcast.48), kind=kOutput, calls=%fused_computation.43 | convolution fusion | flops 510268032 | bytes 3921408 | tf_op jit(solution)/shard_map/dot_general | solution.py:74
  97.7 0.1 copy.53
  97.8 0.0 slice-start
  97.8 0.9 copy.52
  98.7 6.1 %copy.50 = f32[2,8,18,2,3,2,192]{6,5,4,3,2,1,0:T(2,128)} copy(f32[2,8,18,2,3,2,192]{6,2,5,3,4,1,0:T(8,128)} %get-tuple-element.8) | data formatting | bytes 5308416 | tf_op jit(solution)/shard_map/transpose | solution.py:78
  104.8 1.5 %multiply_reduce_fusion = f32[2,8,18,2,3,2]{2,5,3,4,1,0:T(2,128)S(1)} fusion(f32[2,8,18,2,3,2,192]{6,2,5,3,4,1,0:T(8,128)S(1)} %bitcast.44, f32[2,8,18,2,3,2]{2,5,3,4,1,0:T(2,128)S(1)} %copy.53), kind=kLoop, calls=%fused_computation.1 | loop fusion | flops 1987200 | bytes 2681856 | tf_op jit(solution)/shard_map/reduce_sum | solution.py:37
  106.3 0.9 copy.55
  107.3 0.6 rsqrt.21
  107.9 0.0 copy-start.5
  107.9 0.0 copy-start.6
  107.9 5.4 %reshape.129 = f32[3456,192]{1,0:T(8,128)} reshape(f32[2,8,18,2,3,2,192]{6,5,4,3,2,1,0:T(2,128)} %copy.50) | data formatting | bytes 5308416 | tf_op jit(solution)/shard_map/reshape | solution.py:78
  113.3 0.6 div.17
  113.9 3.3 %convolution_convert_fusion = bf16[3456,192]{0,1:T(8,128)(2,1)S(1)} fusion(bf16[192,192]{1,0:T(8,128)(2,1)S(1)} %copy-done, f32[3456,192]{1,0:T(8,128)} %reshape.129, f32[192]{0:T(256)S(1)} %copy-done.5, f32[192]{0:T(256)S(1)} %copy-done.6, f32[3456]{0:T(1024)S(1)} %rsqrt.21, f32[3456]{0:T(1024)S(1)} %div.17), kind=kOutput, calls=%fused_computation | convolution fusion | flops 258785280 | bytes 4084224 | tf_op jit(solution)/shard_map/dot_general | solution.py:82
  117.2 2.2 %copy.56 = bf16[3456,192]{1,0:T(8,128)(2,1)} copy(bf16[3456,192]{0,1:T(8,128)(2,1)S(1)} %convolution_convert_fusion) | data formatting | bytes 2654208 | tf_op jit(solution)/shard_map/convert_element_type | solution.py:85
  119.4 2.8 %reshape.130 = bf16[2,8,36,6,192]{4,3,2,1,0:T(8,128)(2,1)S(1)} reshape(bf16[3456,192]{1,0:T(8,128)(2,1)} %copy.56) | data formatting | bytes 2654208 | tf_op jit(solution)/shard_map/reshape | solution.py:85
  122.3 3.2 %collective-permute-start.2 = (bf16[2,8,1,6,192]{4,3,2,1,0:T(8,128)(2,1)S(1)}, bf16[2,8,1,6,192]{4,3,2,1,0:T(8,128)(2,1)S(1)}, u32[]{:S(2)}, u32[]{:S(2)}) collective-permute-start(bf16[2,8,1,6,192]{4,3,2,1,0:T(8,128)(2,1)S(1)} %constant_dynamic-slice_fusion), channel_id=1, source_target_pairs={{0,2},{2,4},{4,6},{6,8},{8,10},{10,12},{12,14},{1,3},{3,5},{5,7},{... | collective-permute-start | bytes 110600 | tf_op jit(solution)/shard_map/ppermute | solution.py:16
  125.5 1.9 %copy.58 = bf16[2,8,36,6,192]{4,1,3,2,0:T(8,128)(2,1)S(1)} copy(bf16[2,8,36,6,192]{4,3,2,1,0:T(8,128)(2,1)S(1)} %reshape.130) | data formatting | bytes 2654208 | tf_op jit(solution)/shard_map/reshape | solution.py:85
  127.4 0.0 collective-permute-done.2
  127.4 0.3 fusion.16
  127.8 0.5 collective-permute-start.3
  128.3 0.1 slice.31
  128.4 11.2 %collective-permute-done.3 = bf16[2,8,34,1,192]{4,1,3,2,0:T(8,128)(2,1)S(1)} collective-permute-done((bf16[2,8,34,1,192]{4,1,3,2,0:T(8,128)(2,1)S(1)}, bf16[2,8,34,1,192]{4,1,3,2,0:T(8,128)(2,1)S(1)}, u32[]{:S(2)}, u32[]{:S(2)}) %collective-permute-start.3) | collective-permute-done | bytes 208928 | tf_op jit(solution)/shard_map/ppermute | solution.py:10
  139.5 1.5 %maximum_select_fusion = bf16[2,8,34,6,192]{4,1,3,2,0:T(8,128)(2,1)} fusion(bf16[2,8,34,5,192]{4,1,3,2,0:T(8,128)(2,1)S(1)} %slice.31, bf16[2,8,34,1,192]{4,1,3,2,0:T(8,128)(2,1)S(1)} %collective-permute-done.3, pred[34]{0:T(512)(128)(4,1)S(1)} %iota_compare_fusion.1), kind=kLoop, calls=%fused_computation.25 | loop fusion | flops 1253376 | bytes 2506786 | tf_op jit(solution)/shard_map/jit(_where)/select_n | solution.py:96
  (26 shorter events, 0.2 us)
Async XLA Ops:
  0.0 113.9 %copy-start = (bf16[192,192]{1,0:T(8,128)(2,1)S(1)}, bf16[192,192]{1,0:T(8,128)(2,1)}, u32[]{:S(2)}) copy-start(bf16[192,192]{1,0:T(8,128)(2,1)} %param.17) | copy-start | bytes 221188
  1.4 11.3 %all-to-all-start = ((bf16[8,6,384]{2,1,0:T(8,128)(2,1)}), bf16[8,6,384]{2,1,0:T(8,128)(2,1)S(1)}, u32[]{:S(2)}, u32[]{:S(2)}) async-start(bf16[8,6,384]{2,1,0:T(8,128)(2,1)} %broadcast_in_dim.76), calls=%async_computation | async-start | bytes 98304 | tf_op jit(solution)/shard_map/all_to_all | solution.py:27
  13.9 8.8 %all-to-all-start.2 = ((bf16[8,3,768]{2,1,0:T(4,128)(2,1)}), bf16[8,3,768]{2,1,0:T(4,128)(2,1)S(1)}, u32[]{:S(2)}, u32[]{:S(2)}) async-start(bf16[8,3,768]{2,1,0:T(4,128)(2,1)} %broadcast_in_dim.78), calls=%async_computation.2 | async-start | bytes 98304 | tf_op jit(solution)/shard_map/all_to_all | solution.py:27
  23.6 36.7 %all-to-all-start.1 = ((bf16[16,48,384]{2,1,0:T(8,128)(2,1)}), bf16[16,48,384]{2,1,0:T(8,128)(2,1)}, u32[]{:S(2)}, u32[]{:S(2)}) async-start(bf16[16,48,384]{2,1,0:T(8,128)(2,1)} %broadcast_in_dim.77), calls=%async_computation.1 | async-start | bytes 1179648 | tf_op jit(solution)/shard_map/all_to_all | solution.py:27
  36.3 15.8 %collective-permute-start = (bf16[2,8,34,1,192]{4,1,3,2,0:T(8,128)(2,1)}, bf16[2,8,34,1,192]{4,1,3,2,0:T(8,128)(2,1)S(1)}, u32[]{:S(2)}, u32[]{:S(2)}) collective-permute-start(bf16[2,8,34,1,192]{4,1,3,2,0:T(8,128)(2,1)} %slice.29), channel_id=1, source_target_pairs={{16,0},{32,16},{48,32},{64,48},{80,64},{96,80},{112,96},{128,112},... | collective-permute-start | bytes 626696 | tf_op jit(solution)/shard_map/ppermute | solution.py:10
  43.1 13.9 %copy-start.3 = (f32[768]{0:T(1024)S(1)}, f32[768]{0:T(1024)}, u32[]{:S(2)}) copy-start(f32[768]{0:T(1024)} %param.11) | copy-start | bytes 9220
  43.1 14.0 %copy-start.4 = (f32[768]{0:T(1024)S(1)}, f32[768]{0:T(1024)}, u32[]{:S(2)}) copy-start(f32[768]{0:T(1024)} %param.12) | copy-start | bytes 9220
  52.1 5.8 %collective-permute-start.1 = (bf16[2,8,1,6,192]{4,1,3,2,0:T(8,128)(2,1)S(1)}, bf16[2,8,1,6,192]{4,1,3,2,0:T(8,128)(2,1)S(1)}, u32[]{:S(2)}, u32[]{:S(2)}) collective-permute-start(bf16[2,8,1,6,192]{4,1,3,2,0:T(8,128)(2,1)S(1)} %pad_maximum_fusion), channel_id=1, source_target_pairs={{2,0},{4,2},{6,4},{8,6},{10,8},{12,10},{14,12},{3,1},{5,3},{7,5},{... | collective-permute-start | bytes 110600 | tf_op jit(solution)/shard_map/ppermute | solution.py:16
  57.8 0.6 copy-start.2
  59.9 0.8 copy-start.1
  61.5 31.2 %all-to-all-start.3 = ((bf16[16,24,768]{2,1,0:T(8,128)(2,1)}), bf16[16,24,768]{2,1,0:T(8,128)(2,1)}, u32[]{:S(2)}, u32[]{:S(2)}) async-start(bf16[16,24,768]{2,1,0:T(8,128)(2,1)} %broadcast_in_dim.79), calls=%async_computation.3 | async-start | bytes 1179648 | tf_op jit(solution)/shard_map/all_to_all | solution.py:27
  97.8 7.0 %slice-start = ((s8[4718592]{0:T(1024)(128)(4,1)}), s8[524288]{0:T(1024)(128)(4,1)S(1)}, s32[]{:S(2)}) async-start(s8[4718592]{0:T(1024)(128)(4,1)} %bitcast.43), calls=%async_computation.4 | async-start | bytes 1048576
  98.7 6.1 %slice-start.1 = ((s8[4718592]{0:T(1024)(128)(4,1)}), s8[4194304]{0:T(1024)(128)(4,1)S(1)}, s32[]{:S(2)}) async-start(s8[4718592]{0:T(1024)(128)(4,1)} %bitcast.43), calls=%async_computation.5 | async-start | bytes 8388608
  107.9 6.1 %copy-start.5 = (f32[192]{0:T(256)S(1)}, f32[192]{0:T(256)}, u32[]{:S(2)}) copy-start(f32[192]{0:T(256)} %param.16) | copy-start | bytes 2308
  107.9 6.1 %copy-start.6 = (f32[192]{0:T(256)S(1)}, f32[192]{0:T(256)}, u32[]{:S(2)}) copy-start(f32[192]{0:T(256)} %param.15) | copy-start | bytes 2308
  122.3 5.1 %collective-permute-start.2 = (bf16[2,8,1,6,192]{4,3,2,1,0:T(8,128)(2,1)S(1)}, bf16[2,8,1,6,192]{4,3,2,1,0:T(8,128)(2,1)S(1)}, u32[]{:S(2)}, u32[]{:S(2)}) collective-permute-start(bf16[2,8,1,6,192]{4,3,2,1,0:T(8,128)(2,1)S(1)} %constant_dynamic-slice_fusion), channel_id=1, source_target_pairs={{0,2},{2,4},{4,6},{6,8},{8,10},{10,12},{12,14},{1,3},{3,5},{5,7},{... | collective-permute-start | bytes 110600 | tf_op jit(solution)/shard_map/ppermute | solution.py:16
  127.8 11.8 %collective-permute-start.3 = (bf16[2,8,34,1,192]{4,1,3,2,0:T(8,128)(2,1)S(1)}, bf16[2,8,34,1,192]{4,1,3,2,0:T(8,128)(2,1)S(1)}, u32[]{:S(2)}, u32[]{:S(2)}) collective-permute-start(bf16[2,8,34,1,192]{4,1,3,2,0:T(8,128)(2,1)S(1)} %slice.30), channel_id=1, source_target_pairs={{240,0},{0,16},{16,32},{32,48},{48,64},{64,80},{80,96},{96,112},{1... | collective-permute-start | bytes 626696 | tf_op jit(solution)/shard_map/ppermute | solution.py:10
where the time goes:
time: 142 us; the launch traced here: 141 us
  starting transfers between devices  43.7 us (31%)
  waiting for transfers between devices  41.1 us (29%)
  local copies, waits for them, and re-layouts  35.8 us (25%)
  matrix products  8.79 us (6%)
  other arithmetic  8.3 us (6%)
  between operations  3.46 us (2%)
    all_to_all x4, starting transfers between devices, from_everyone(): return lax.all_to_all(copies, axis, split_axis=0, concat_axis=0, tiled=True)  31.5 us
    all_to_all x4, waiting for transfers between devices, from_everyone(): return lax.all_to_all(copies, axis, split_axis=0, concat_axis=0, tiled=True)  21.1 us
    ppermute x2, waiting for transfers between devices, shifted(): return lax.ppermute(block, axis, route)  20 us
    ppermute x2, starting transfers between devices, passed_along(): return lax.ppermute(block, axis, route)  6.7 us
    transpose x1, local copies, waits for them, and re-layouts, body(): grown.transpose(0, 1, 2, 4, 3, 5, 6)  6.1 us
    ppermute x2, starting transfers between devices, shifted(): return lax.ppermute(block, axis, route)  5.43 us
    reshape x1, local copies, waits for them, and re-layouts, body(): grown.transpose(0, 1, 2, 4, 3, 5, 6)  5.43 us
    reshape x2, local copies, waits for them, and re-layouts, body(): fine_out.astype(jnp.bfloat16)  4.71 us
  transfers between devices with their start and end apart: 8, of which 5 were waited for; matrix products, arithmetic and copies ran while one was open for 11% of the time, Pallas kernels for 0%

commit v1 on v0

v1 whole, which is shorter than its diff:
```python
import functools

import jax
import jax.numpy as jnp
from jax import lax
from jax.experimental import pallas as pl
from jax.experimental.pallas import tpu as pltpu
from jax.sharding import PartitionSpec as P

MESH = pl.DeviceIdType.MESH
MEMBERS, LEVELS, SLOTS, COLS, C = 2, 8, 34, 6, 192
EXT = SLOTS + 2
HALF = EXT // 2
NZ = 8
PIECES = 3
BF = jnp.bfloat16
F32 = jnp.float32


def exchange(
    band_ref, tok_hbm, down_hbm, up_hbm,
    wd, wu, west, east, north, south,
    tok, last, own_d, own_u, got_d, got_u, flat_d, flat_u,
    load_sem, s1_send, s1_recv, ring_send, ring_recv, pair_send, pair_recv,
    col_send, col_recv, row_send, row_recv,
):
    lon, lat, mem = lax.axis_index("lon"), lax.axis_index("lat"), lax.axis_index("mem")
    z, yh = lon // 2, lon % 2
    core, xx = lat % 2, lat // 2

    def at(lon_, lat_, mem_):
        return (lon_, lat_, mem_)

    def other(yh_):
        return 2 * z + yh_

    loads = [
        pltpu.make_async_copy(down_hbm, own_d, load_sem.at[0]),
        pltpu.make_async_copy(up_hbm, own_u, load_sem.at[1]),
        pltpu.make_async_copy(tok_hbm, tok, load_sem.at[2]),
    ]
    for load in loads:
        load.start()

    lon_w, lon_e = (lon + 15) % 16, (lon + 1) % 16
    lat_n, lat_s = (lat + 7) % 8, (lat + 1) % 8
    up_z = ((z + 1) % NZ) * 2 + yh
    dn_z = ((z + NZ - 1) % NZ) * 2 + yh
    barrier = pltpu.get_barrier_semaphore()

    def greet(where):
        pl.semaphore_signal(barrier, inc=1, device_id=where, device_id_type=MESH)

    for d in range(1, 8):
        greet(at(lon, (lat + d) % 8, mem))
    for d in range(8):
        greet(at(other(1 - yh), (lat + d) % 8, 1 - mem))
    for where in (
        at(up_z, lat, mem), at(dn_z, lat, mem), at(lon_w, lat, mem), at(lon_e, lat, mem),
        at(lon_w, lat_n, mem), at(lon_w, lat_s, mem), at(lon_e, lat_n, mem), at(lon_e, lat_s, mem),
    ):
        greet(where)
    loads[0].wait()
    loads[1].wait()
    pl.semaphore_wait(barrier, 23)

    me = yh * 8 + lat

    def copy(src, dst, ssem, rsem, where):
        return pltpu.make_async_remote_copy(
            src_ref=src, dst_ref=dst, send_sem=ssem, recv_sem=rsem,
            device_id=where, device_id_type=MESH,
        )

    def stage_one(src, got, kind, base):
        out = []
        for d in range(4):
            lat_t = 2 * ((xx + d) % 4) + kind
            out.append((d, 0, copy(src, got.at[me], s1_send.at[base + d], s1_recv.at[me], at(lon, lat_t, mem))))
            out.append((d, 1, copy(src, got.at[me], s1_send.at[base + 4 + d], s1_recv.at[me], at(other(1 - yh), lat_t, 1 - mem))))
        return out

    sends = [(0, s) for s in stage_one(own_d, got_d, 0, 0)] + [(1, s) for s in stage_one(own_u, got_u, 1, 8)]
    for kind, (d, far, cp) in sends:
        if d == 0 and far == 0:
            @pl.when(core != kind)
            def _():
                cp.start()
        else:
            cp.start()

    loads[2].wait()
    cols = [
        copy(tok.at[:, :, 0], east, col_send.at[0], col_recv.at[0], at(lon_w, lat, mem)),
        copy(tok.at[:, :, COLS - 1], west, col_send.at[1], col_recv.at[1], at(lon_e, lat, mem)),
    ]
    for cp in cols:
        cp.start()

    live = band_ref[0, 1] - band_ref[0, 0]
    last[...] = tok[:, pl.ds(jnp.clip(live - 1, 0, SLOTS - 1), 1)].reshape(MEMBERS, COLS, LEVELS, C)
    to_next = [
        copy(last, north.at[:, 1 : COLS + 1], row_send.at[0], row_recv.at[0], at(lon, lat_s, mem)),
        copy(last.at[:, 0], north.at[:, COLS + 1], row_send.at[1], row_recv.at[1], at(lon_w, lat_s, mem)),
        copy(last.at[:, COLS - 1], north.at[:, 0], row_send.at[2], row_recv.at[2], at(lon_e, lat_s, mem)),
    ]
    to_prev = [
        copy(tok.at[:, 0], south.at[:, 1 : COLS + 1], row_send.at[3], row_recv.at[3], at(lon, lat_n, mem)),
        copy(tok.at[:, 0, 0], south.at[:, COLS + 1], row_send.at[4], row_recv.at[4], at(lon_w, lat_n, mem)),
        copy(tok.at[:, 0, COLS - 1], south.at[:, 0], row_send.at[5], row_recv.at[5], at(lon_e, lat_n, mem)),
    ]

    @pl.when(lat < 7)
    def _():
        for cp in to_next:
            cp.start()

    @pl.when(lat > 0)
    def _():
        for cp in to_prev:
            cp.start()

    @pl.when(lat == 7)
    def _():
        south[...] = jnp.zeros_like(south)

    @pl.when(lat == 0)
    def _():
        north[...] = jnp.zeros_like(north)

    def gather(kind, own, got, flat, full, rows):
        part = 16 * rows // PIECES
        got[pl.ds(me, 1)] = own[...].reshape(1, *own.shape)
        for d in range(1, 16):
            i = (me + d) % 16
            copy(own, got.at[i], s1_send.at[0], s1_recv.at[i], at(lon, lat, mem)).wait_recv()
        for i in range(16):
            flat[rows * i : rows * (i + 1), :] = got[i].astype(F32)
        full[pl.ds(z, 1)] = flat[...].astype(BF).reshape(1, *flat.shape)

        def block(step, way):
            return (z + NZ + (step if way else -step)) % NZ

        def piece(b, k):
            return full.at[b, part * k : part * (k + 1)]

        def ring(step, way, k):
            b = block(step, way)
            return copy(
                piece(b, k), piece(b, k), ring_send.at[way, step, k], ring_recv.at[way, step, k],
                at(dn_z if way else up_z, lat, mem),
            )

        def landed(step, way, k):
            b = block(step + 1, way)
            return copy(
                piece(b, k), piece(b, k), ring_send.at[way, step, k], ring_recv.at[way, step, k],
                at(dn_z if way else up_z, lat, mem),
            )

        def pair(b):
            return copy(full.at[b], full.at[b], pair_send.at[b], pair_recv.at[b], at(lon, lat + 1 - 2 * core, mem))

        steps = (4, 3)
        for k in range(PIECES):
            for way in range(2):
                ring(0, way, k).start()
        pair(z).start()
        for step in range(4):
            for k in range(PIECES):
                for way in range(2):
                    if step < steps[way]:
                        landed(step, way, k).wait_recv()
                        if step + 1 < steps[way]:
                            ring(step + 1, way, k).start()
            for way in range(2):
                if step < steps[way]:
                    pair(block(step + 1, way)).start()
        for step in range(4):
            for k in range(PIECES):
                for way in range(2):
                    if step < steps[way]:
                        ring(step, way, k).wait_send()
        for b in range(NZ):
            pair(b).wait_send()

    def take(full):
        for b in range(NZ):
            copy(full.at[b], full.at[b], pair_send.at[b], pair_recv.at[b], at(lon, lat, mem)).wait_recv()

    @pl.when(core == 0)
    def _():
        gather(0, own_d, got_d, flat_d, wd, 6)
        take(wu)

    @pl.when(core == 1)
    def _():
        gather(1, own_u, got_u, flat_u, wu, 3)
        take(wd)

    for kind, (d, far, cp) in sends:
        if d == 0 and far == 0:
            @pl.when(core != kind)
            def _():
                cp.wait_send()
        else:
            cp.wait_send()
    for cp in cols:
        cp.wait()

    @pl.when(lat < 7)
    def _():
        for cp in to_next:
            cp.wait_send()
        for cp in to_prev:
            cp.wait_recv()

    @pl.when(lat > 0)
    def _():
        for cp in to_prev:
            cp.wait_send()
        for cp in to_next:
            cp.wait_recv()


def run_exchange(band_rows, tok, down, up):
    dma = pltpu.SemaphoreType.DMA
    vmem = pl.BlockSpec(memory_space=pltpu.VMEM)
    anywhere = pl.BlockSpec(memory_space=pl.ANY)
    col = (MEMBERS, SLOTS, LEVELS, C)
    row = (MEMBERS, COLS + 2, LEVELS, C)
    return pl.pallas_call(
        exchange,
        out_shape=[
            jax.ShapeDtypeStruct((NZ, 96, 384), BF),
            jax.ShapeDtypeStruct((NZ, 48, 768), BF),
            jax.ShapeDtypeStruct(col, BF),
            jax.ShapeDtypeStruct(col, BF),
            jax.ShapeDtypeStruct(row, BF),
            jax.ShapeDtypeStruct(row, BF),
        ],
        in_specs=[pl.BlockSpec(memory_space=pltpu.SMEM), anywhere, anywhere, anywhere],
        out_specs=[vmem] * 6,
        scratch_shapes=[
            pltpu.VMEM((MEMBERS, SLOTS, COLS, LEVELS, C), BF),
            pltpu.VMEM((MEMBERS, COLS, LEVELS, C), BF),
            pltpu.VMEM((6, 384), BF),
            pltpu.VMEM((3, 768), BF),
            pltpu.VMEM((16, 6, 384), BF),
            pltpu.VMEM((16, 3, 768), BF),
            pltpu.VMEM((96, 384), F32),
            pltpu.VMEM((48, 768), F32),
            dma((3,)), dma((16,)), dma((16,)),
            dma((2, 4, PIECES)), dma((2, 4, PIECES)), dma((NZ,)), dma((NZ,)),
            dma((2,)), dma((2,)), dma((6,)), dma((6,)),
        ],
        compiler_params=pltpu.CompilerParams(collective_id=0, has_side_effects=True),
        name="exchange",
    )(band_rows, tok, down, up)


GROUP = 6


def patches(
    band_ref, tok_hbm, wd, wu, west, east, north, south, dg, ds, ug, us, mix,
    out_hbm, ext, fine, wu4, load_sem, store_sem,
):
    lat = lax.axis_index("lat")
    shift = jnp.minimum(lat, 1)
    live = band_ref[0, 1] - band_ref[0, 0]
    load = pltpu.make_async_copy(
        tok_hbm, ext.at[:, pl.ds(shift, SLOTS), 1 : COLS + 1], load_sem
    )
    load.start()
    for g in range(4):
        wu4[g] = wu[:, C * g : C * (g + 1)]
    ext[:, pl.ds(shift, SLOTS), 0] = west[...]
    ext[:, pl.ds(shift, SLOTS), COLS + 1] = east[...]
    load.wait()

    @pl.when(lat > 0)
    def _():
        ext[:, 0] = north[...]

    ext[:, pl.ds(jnp.clip(live + shift, 0, EXT - 1), 1)] = south[...].reshape(MEMBERS, 1, COLS + 2, LEVELS, C)

    view = ext.reshape(MEMBERS, HALF, 2, 4, 2, LEVELS, C)
    eps = 1e-05
    stores = []
    for m in range(MEMBERS):
        @pl.loop(0, HALF // GROUP)
        def _(it):
            k0 = it * GROUP
            cells = {}
            total = None
            for q in range(2):
                for p in range(2):
                    x = jnp.concatenate(
                        [view[m, pl.ds(k0, GROUP), p, j, q].reshape(GROUP * LEVELS, C) for j in range(4)], axis=0
                    ).astype(F32)
                    cells[q, p] = x
                    s = jnp.sum(x, axis=1, keepdims=True)
                    total = s if total is None else total + s
            average = total * (1.0 / (4 * C))
            total = None
            for key in cells:
                cells[key] = cells[key] - average
                s = jnp.sum(cells[key] * cells[key], axis=1, keepdims=True)
                total = s if total is None else total + s
            scale = lax.rsqrt(total * (1.0 / (4 * C)) + eps)
            coarse = None
            for q in range(2):
                for p in range(2):
                    g = 2 * q + p
                    normed = (cells[q, p] * scale * dg[g : g + 1, :] + ds[g : g + 1, :]).astype(BF)
                    term = jnp.dot(normed, wd[C * g : C * (g + 1), :], preferred_element_type=F32)
                    coarse = term if coarse is None else coarse + term
            coarse = coarse.astype(BF)
            n = GROUP * LEVELS
            for p in range(2):
                for q in range(2):
                    j0 = 1 - q
                    grown = jnp.dot(coarse[n * j0 : n * (j0 + 3)], wu4[2 * p + q], preferred_element_type=F32)
                    average = jnp.sum(grown, axis=1, keepdims=True) * (1.0 / C)
                    grown = grown - average
                    spread = jnp.sum(grown * grown, axis=1, keepdims=True) * (1.0 / C)
                    normed = (grown * lax.rsqrt(spread + eps) * ug[...] + us[...]).astype(BF)
                    done = jnp.dot(normed, mix[...], preferred_element_type=F32).astype(BF)
                    done = done.reshape(3, GROUP, LEVELS, C)
                    rows = 2 * (k0 + lax.broadcasted_iota(jnp.int32, (GROUP, LEVELS, C), 0)) + p
                    keep = rows < live + shift
                    for j in range(3):
                        fine[m, pl.ds(k0, GROUP), p, 2 * (j + j0) + q - 1] = jnp.where(keep, done[j], jnp.zeros_like(done[j]))
        rows_out = fine.reshape(MEMBERS, EXT, COLS, LEVELS, C)
        store = pltpu.make_async_copy(rows_out.at[m, pl.ds(shift, SLOTS)], out_hbm.at[m], store_sem.at[m])
        store.start()
        stores.append(store)
    for store in stores:
        store.wait()


def run_patches(band_rows, tok, wd, wu, west, east, north, south, dg, ds, ug, us, mix):
    vmem = pl.BlockSpec(memory_space=pltpu.VMEM)
    anywhere = pl.BlockSpec(memory_space=pl.ANY)
    return pl.pallas_call(
        patches,
        out_shape=jax.ShapeDtypeStruct((MEMBERS, SLOTS, COLS, LEVELS, C), BF),
        in_specs=[pl.BlockSpec(memory_space=pltpu.SMEM), anywhere] + [vmem] * 11,
        out_specs=anywhere,
        scratch_shapes=[
            pltpu.VMEM((MEMBERS, EXT, COLS + 2, LEVELS, C), BF),
            pltpu.VMEM((MEMBERS, HALF, 2, COLS, LEVELS, C), BF),
            pltpu.VMEM((4, 2 * C, C), BF),
            pltpu.SemaphoreType.DMA,
            pltpu.SemaphoreType.DMA((MEMBERS,)),
        ],
        name="patches",
    )(band_rows, tok, wd, wu, west, east, north, south, dg, ds, ug, us, mix)


def body(
    tokens, band_rows, down_gain, down_shift, down_weight, up_weight, up_gain, up_shift, mix_weight
):
    tok = tokens.transpose(0, 2, 3, 1, 4)
    wd, wu, west, east, north, south = run_exchange(band_rows, tok, down_weight, up_weight)
    out = run_patches(
        band_rows, tok, wd.reshape(4 * C, 2 * C), wu.reshape(2 * C, 4 * C), west, east, north, south,
        down_gain.reshape(4, C), down_shift.reshape(4, C), up_gain.reshape(1, C), up_shift.reshape(1, C), mix_weight,
    )
    return out.transpose(0, 3, 1, 2, 4)


def solution(mesh):
    return jax.shard_map(
        body,
        mesh=mesh,
        in_specs=(
            P("mem", None, "lat", "lon", None),
            P("lat", None),
            P(),
            P(),
            P(("lon", "lat"), None),
            P(("lon", "lat"), None),
            P(),
            P(),
            P(),
        ),
        out_specs=P("mem", None, "lat", "lon", None),
        check_vma=False,
    )
```

time: 142 us -> 62.2 us (0.44)
  the two profiles are of different devices: /device:TPU:1 before, /device:TPU:3 now
where the time goes in v1:
time: 62.2 us; the launch traced here: 62 us
  Pallas kernels  59.3 us (95%)
  local copies, waits for them, and re-layouts  2.71 us (4%)
    pallas_call x1, Pallas kernels, run_exchange(): pl.pallas_call(exchange, out_shape=[jax.ShapeDtypeStruct((NZ, 96, 384), B...  42.5 us
    pallas_call x1, Pallas kernels, run_patches(): pl.pallas_call(patches, out_shape=jax.ShapeDtypeStruct((MEMBERS, SLOTS, C...  16.8 us
    reshape x1, local copies, waits for them, and re-layouts, body(): down_shift.reshape(4, C)  1.36 us
    reshape x1, local copies, waits for them, and re-layouts, body(): down_gain.reshape(4, C)  1.35 us

profile of v1, /device:TPU:3, one launch (start us, length us, event | category | flops | bytes accessed | tf_op | source)
XLA Modules:
  0.0 62.0 jit_solution(14826393387939245374)
XLA Ops:
  0.0 1.3 %reshape.20.dg = f32[4,192]{1,0:T(4,128)} reshape(f32[768]{0:T(1024)} %param.11) | data formatting | bytes 6144 | tf_op jit(solution)/shard_map/reshape | solution.py:369
  1.4 1.4 %reshape.21.ds = f32[4,192]{1,0:T(4,128)} reshape(f32[768]{0:T(1024)} %param.12) | data formatting | bytes 6144 | tf_op jit(solution)/shard_map/reshape | solution.py:369
  2.7 42.5 %exchange.1 = (bf16[8,96,384]{2,1,0:T(8,128)(2,1)}, bf16[8,48,768]{2,1,0:T(8,128)(2,1)}, bf16[2,34,8,192]{3,2,1,0:T(8,128)(2,1)}, bf16[2,34,8,192]{3,2,1,0:T(8,1...) custom-call(s32[1,2]{1,0:T(1,128)} %band_ref.3, bf16[2,34,6,8,192]{4,3,2,1,0:T(8,128)(2,1)} %bitcast.6, ...), custom_call_target="tpu_custom_call" | custom-call | tf_op jit(solution)/shard_map/exchange/pallas_call | solution.py:232
  45.2 16.8 %patches.1 = bf16[2,34,6,8,192]{4,3,2,1,0:T(8,128)(2,1)} custom-call(s32[1,2]{1,0:T(1,128)} %band_ref.3, bf16[2,34,6,8,192]{4,3,2,1,0:T(8,128)(2,1)} %bitcast.7, bf16[768,384]{1,0:T(8,128)(2,1)} %bitcast.8, bf16[384,768]{1,0:T(8,128)(2,1)} %bitcast.9, bf16[2,34,8,192]{3,2,1,0:T(8,128)(2,1)} %get-tuple-element.13.west, ...), custom_call_target="tpu_custom_call" | custom-call | tf_op jit(solution)/shard_map/patches/pallas_call | solution.py:346

commit v2 on v1

--- a/solution.py
+++ b/solution.py
@@ -18,10 +18,10 @@
 
 
 def exchange(
-    band_ref, tok_hbm, down_hbm, up_hbm,
+    band_ref, tok, own_d, own_u,
     wd, wu, west, east, north, south,
-    tok, last, own_d, own_u, got_d, got_u, flat_d, flat_u,
-    load_sem, s1_send, s1_recv, ring_send, ring_recv, pair_send, pair_recv,
+    last, got_d, got_u, flat_d, flat_u,
+    s1_send, s1_recv, ring_send, ring_recv, pair_send, pair_recv,
     col_send, col_recv, row_send, row_recv,
 ):
     lon, lat, mem = lax.axis_index("lon"), lax.axis_index("lat"), lax.axis_index("mem")
@@ -33,14 +33,6 @@
 
     def other(yh_):
         return 2 * z + yh_
-
-    loads = [
-        pltpu.make_async_copy(down_hbm, own_d, load_sem.at[0]),
-        pltpu.make_async_copy(up_hbm, own_u, load_sem.at[1]),
-        pltpu.make_async_copy(tok_hbm, tok, load_sem.at[2]),
-    ]
-    for load in loads:
-        load.start()
 
     lon_w, lon_e = (lon + 15) % 16, (lon + 1) % 16
     lat_n, lat_s = (lat + 7) % 8, (lat + 1) % 8
@@ -60,8 +52,6 @@
         at(lon_w, lat_n, mem), at(lon_w, lat_s, mem), at(lon_e, lat_n, mem), at(lon_e, lat_s, mem),
     ):
         greet(where)
-    loads[0].wait()
-    loads[1].wait()
     pl.semaphore_wait(barrier, 23)
 
     me = yh * 8 + lat
@@ -89,7 +79,6 @@
         else:
             cp.start()
 
-    loads[2].wait()
     cols = [
         copy(tok.at[:, :, 0], east, col_send.at[0], col_recv.at[0], at(lon_w, lat, mem)),
         copy(tok.at[:, :, COLS - 1], west, col_send.at[1], col_recv.at[1], at(lon_e, lat, mem)),
@@ -226,7 +215,6 @@
 def run_exchange(band_rows, tok, down, up):
     dma = pltpu.SemaphoreType.DMA
     vmem = pl.BlockSpec(memory_space=pltpu.VMEM)
-    anywhere = pl.BlockSpec(memory_space=pl.ANY)
     col = (MEMBERS, SLOTS, LEVELS, C)
     row = (MEMBERS, COLS + 2, LEVELS, C)
     return pl.pallas_call(
@@ -239,22 +227,19 @@
             jax.ShapeDtypeStruct(row, BF),
             jax.ShapeDtypeStruct(row, BF),
         ],
-        in_specs=[pl.BlockSpec(memory_space=pltpu.SMEM), anywhere, anywhere, anywhere],
+        in_specs=[pl.BlockSpec(memory_space=pltpu.SMEM), vmem, vmem, vmem],
         out_specs=[vmem] * 6,
         scratch_shapes=[
-            pltpu.VMEM((MEMBERS, SLOTS, COLS, LEVELS, C), BF),
             pltpu.VMEM((MEMBERS, COLS, LEVELS, C), BF),
-            pltpu.VMEM((6, 384), BF),
-            pltpu.VMEM((3, 768), BF),
             pltpu.VMEM((16, 6, 384), BF),
             pltpu.VMEM((16, 3, 768), BF),
             pltpu.VMEM((96, 384), F32),
             pltpu.VMEM((48, 768), F32),
-            dma((3,)), dma((16,)), dma((16,)),
+            dma((16,)), dma((16,)),
             dma((2, 4, PIECES)), dma((2, 4, PIECES)), dma((NZ,)), dma((NZ,)),
             dma((2,)), dma((2,)), dma((6,)), dma((6,)),
         ],
-        compiler_params=pltpu.CompilerParams(collective_id=0, has_side_effects=True),
+        compiler_params=pltpu.CompilerParams(collective_id=0, has_side_effects=True, vmem_limit_bytes=24 << 20),
         name="exchange",
     )(band_rows, tok, down, up)
 
@@ -263,21 +248,17 @@
 
 
 def patches(
-    band_ref, tok_hbm, wd, wu, west, east, north, south, dg, ds, ug, us, mix,
-    out_hbm, ext, fine, wu4, load_sem, store_sem,
+    band_ref, tok, wd, wu, west, east, north, south, dg, ds, ug, us, mix,
+    out_hbm, ext, fine, wu4, store_sem,
 ):
     lat = lax.axis_index("lat")
     shift = jnp.minimum(lat, 1)
     live = band_ref[0, 1] - band_ref[0, 0]
-    load = pltpu.make_async_copy(
-        tok_hbm, ext.at[:, pl.ds(shift, SLOTS), 1 : COLS + 1], load_sem
-    )
-    load.start()
     for g in range(4):
         wu4[g] = wu[:, C * g : C * (g + 1)]
     ext[:, pl.ds(shift, SLOTS), 0] = west[...]
     ext[:, pl.ds(shift, SLOTS), COLS + 1] = east[...]
-    load.wait()
+    ext[:, pl.ds(shift, SLOTS), 1 : COLS + 1] = tok[...]
 
     @pl.when(lat > 0)
     def _():
@@ -287,6 +268,8 @@
 
     view = ext.reshape(MEMBERS, HALF, 2, 4, 2, LEVELS, C)
     eps = 1e-05
+    gains, shifts = dg[...].reshape(1, 4 * C), ds[...].reshape(1, 4 * C)
+    fine_gain, fine_shift = ug[...].reshape(1, C), us[...].reshape(1, C)
     stores = []
     for m in range(MEMBERS):
         @pl.loop(0, HALF // GROUP)
@@ -313,7 +296,7 @@
             for q in range(2):
                 for p in range(2):
                     g = 2 * q + p
-                    normed = (cells[q, p] * scale * dg[g : g + 1, :] + ds[g : g + 1, :]).astype(BF)
+                    normed = (cells[q, p] * scale * gains[:, C * g : C * (g + 1)] + shifts[:, C * g : C * (g + 1)]).astype(BF)
                     term = jnp.dot(normed, wd[C * g : C * (g + 1), :], preferred_element_type=F32)
                     coarse = term if coarse is None else coarse + term
             coarse = coarse.astype(BF)
@@ -325,7 +308,7 @@
                     average = jnp.sum(grown, axis=1, keepdims=True) * (1.0 / C)
                     grown = grown - average
                     spread = jnp.sum(grown * grown, axis=1, keepdims=True) * (1.0 / C)
-                    normed = (grown * lax.rsqrt(spread + eps) * ug[...] + us[...]).astype(BF)
+                    normed = (grown * lax.rsqrt(spread + eps) * fine_gain + fine_shift).astype(BF)
                     done = jnp.dot(normed, mix[...], preferred_element_type=F32).astype(BF)
                     done = done.reshape(3, GROUP, LEVELS, C)
                     rows = 2 * (k0 + lax.broadcasted_iota(jnp.int32, (GROUP, LEVELS, C), 0)) + p
@@ -346,15 +329,15 @@
     return pl.pallas_call(
         patches,
         out_shape=jax.ShapeDtypeStruct((MEMBERS, SLOTS, COLS, LEVELS, C), BF),
-        in_specs=[pl.BlockSpec(memory_space=pltpu.SMEM), anywhere] + [vmem] * 11,
+        in_specs=[pl.BlockSpec(memory_space=pltpu.SMEM), vmem] + [vmem] * 11,
         out_specs=anywhere,
         scratch_shapes=[
             pltpu.VMEM((MEMBERS, EXT, COLS + 2, LEVELS, C), BF),
             pltpu.VMEM((MEMBERS, HALF, 2, COLS, LEVELS, C), BF),
             pltpu.VMEM((4, 2 * C, C), BF),
-            pltpu.SemaphoreType.DMA,
             pltpu.SemaphoreType.DMA((MEMBERS,)),
         ],
+        compiler_params=pltpu.CompilerParams(vmem_limit_bytes=24 << 20),
         name="patches",
     )(band_rows, tok, wd, wu, west, east, north, south, dg, ds, ug, us, mix)
 
@@ -366,7 +349,7 @@
     wd, wu, west, east, north, south = run_exchange(band_rows, tok, down_weight, up_weight)
     out = run_patches(
         band_rows, tok, wd.reshape(4 * C, 2 * C), wu.reshape(2 * C, 4 * C), west, east, north, south,
-        down_gain.reshape(4, C), down_shift.reshape(4, C), up_gain.reshape(1, C), up_shift.reshape(1, C), mix_weight,
+        down_gain, down_shift, up_gain, up_shift, mix_weight,
     )
     return out.transpose(0, 3, 1, 2, 4)
 

time: 62.2 us -> 60 us (0.965)
  Pallas kernels: 59.3 us -> 56.2 us
  local copies, waits for them, and re-layouts: 2.71 us -> 3.51 us
    unnamed x0 -> x18, local copies, waits for them, and re-layouts: none -> 3.51 us
    reshape x2 -> x0, local copies, waits for them, and re-layouts: 2.71 us -> none  [the longest x1 1.36 us: body(): down_shift.reshape(4, C)]
    pallas_call x1, Pallas kernels: 16.8 us -> 15 us  [run_patches(): pl.pallas_call(patches, out_shape=jax.ShapeDtypeStruct((MEMBERS, SLOTS, C...]
    pallas_call x1, Pallas kernels: 42.5 us -> 41.2 us  [run_exchange(): pl.pallas_call(exchange, out_shape=[jax.ShapeDtypeStruct((NZ, 96, 384), B...]
where the time goes in v2:
time: 60 us; the launch traced here: 59.8 us
  Pallas kernels  56.2 us (94%)
  local copies, waits for them, and re-layouts  3.51 us (6%)
    pallas_call x1, Pallas kernels, run_exchange(): pl.pallas_call(exchange, out_shape=[jax.ShapeDtypeStruct((NZ, 96, 384), B...  41.2 us
    pallas_call x1, Pallas kernels, run_patches(): pl.pallas_call(patches, out_shape=jax.ShapeDtypeStruct((MEMBERS, SLOTS, C...  15 us
    unnamed x18, local copies, waits for them, and re-layouts  3.51 us

profile of v2, /device:TPU:3, one launch (start us, length us, event | category | flops | bytes accessed | tf_op | source)
XLA Modules:
  0.0 59.8 jit_solution(8368644370484838193)
XLA Ops:
  0.0 0.0 copy-start.7
  0.0 0.0 copy-start
  0.0 1.5 %copy-done = bf16[2,8,34,6,192]{4,1,3,2,0:T(8,128)(2,1)S(1)} copy-done((bf16[2,8,34,6,192]{4,1,3,2,0:T(8,128)(2,1)S(1)}, bf16[2,8,34,6,192]{4,1,3,2,0:T(8,128)(2,1)}, u32[]{:S(2)}) %copy-start) | copy-done | bytes 1253400
  1.5 0.0 copy-start.2
  1.5 0.7 %copy-done.2 = bf16[6,384]{1,0:T(8,128)(2,1)S(1)} copy-done((bf16[6,384]{1,0:T(8,128)(2,1)S(1)}, bf16[6,384]{1,0:T(8,128)(2,1)}, u32[]{:S(2)}) %copy-start.2) | copy-done | bytes 4632
  2.2 0.0 copy-start.3
  2.2 0.7 %copy-done.3 = bf16[3,768]{1,0:T(4,128)(2,1)S(1)} copy-done((bf16[3,768]{1,0:T(4,128)(2,1)S(1)}, bf16[3,768]{1,0:T(4,128)(2,1)}, u32[]{:S(2)}) %copy-start.3) | copy-done | bytes 4632
  2.8 0.0 copy-start.6
  2.8 0.7 %copy-done.6 = s32[1,2]{1,0:T(1,128)S(1)} copy-done((s32[1,2]{1,0:T(1,128)S(1)}, s32[1,2]{1,0:T(1,128)}, u32[]{:S(2)}) %copy-start.6) | copy-done | bytes 32
  3.5 0.0 copy-start.1
  3.5 0.0 copy-start.4
  3.5 0.0 copy-start.5
  3.5 0.0 copy-start.8
  3.5 41.2 %exchange.1 = (bf16[8,96,384]{2,1,0:T(8,128)(2,1)S(1)}, bf16[8,48,768]{2,1,0:T(8,128)(2,1)S(1)}, bf16[2,34,8,192]{3,2,1,0:T(8,128)(2,1)S(1)}, bf16[2,34,8,192]{3...) custom-call(s32[1,2]{1,0:T(1,128)S(1)} %copy-done.6, ...), custom_call_target="tpu_custom_call" | custom-call | tf_op jit(solution)/shard_map/exchange/pallas_call | solution.py:220
  44.7 0.0 copy-done.7
  44.7 0.0 copy-done.1
  44.7 0.0 copy-done.4
  44.7 0.0 copy-done.5
  44.8 0.0 copy-done.8
  44.8 15.0 %patches.1 = bf16[2,34,6,8,192]{4,3,2,1,0:T(8,128)(2,1)} custom-call(s32[1,2]{1,0:T(1,128)S(1)} %copy-done.6, bf16[2,34,6,8,192]{4,3,2,1,0:T(8,128)(2,1)S(1)} %bitcast.5, bf16[768,384]{1,0:T(8,128)(2,1)S(1)} %bitcast.6, bf16[384,768]{1,0:T(8,128)(2,1)S(1)} %bitcast.7, bf16[2,34,8,192]{3,2,1,0:T(8,128)(2,1)S(1)} %get-tuple-element.13.west, ...), custom_call_target="tpu_custom_call" | custom-call | tf_op jit(solution)/shard_map/patches/pallas_call | solution.py:329
Async XLA Ops:
  0.0 44.7 %copy-start.7 = (f32[192]{0:T(256)S(1)}, f32[192]{0:T(256)}, u32[]{:S(2)}) copy-start(f32[192]{0:T(256)} %ug.1) | copy-start | bytes 2308
  0.0 1.5 %copy-start = (bf16[2,8,34,6,192]{4,1,3,2,0:T(8,128)(2,1)S(1)}, bf16[2,8,34,6,192]{4,1,3,2,0:T(8,128)(2,1)}, u32[]{:S(2)}) copy-start(bf16[2,8,34,6,192]{4,1,3,2,0:T(8,128)(2,1)} %param.9) | copy-start | bytes 3760132
  1.5 0.7 %copy-start.2 = (bf16[6,384]{1,0:T(8,128)(2,1)S(1)}, bf16[6,384]{1,0:T(8,128)(2,1)}, u32[]{:S(2)}) copy-start(bf16[6,384]{1,0:T(8,128)(2,1)} %own_d.1) | copy-start | bytes 13828
  2.2 0.7 %copy-start.3 = (bf16[3,768]{1,0:T(4,128)(2,1)S(1)}, bf16[3,768]{1,0:T(4,128)(2,1)}, u32[]{:S(2)}) copy-start(bf16[3,768]{1,0:T(4,128)(2,1)} %own_u.1) | copy-start | bytes 13828
  2.8 0.7 %copy-start.6 = (s32[1,2]{1,0:T(1,128)S(1)}, s32[1,2]{1,0:T(1,128)}, u32[]{:S(2)}) copy-start(s32[1,2]{1,0:T(1,128)} %band_ref.3) | copy-start | bytes 28
  3.5 41.2 %copy-start.1 = (bf16[192,192]{1,0:T(8,128)(2,1)S(1)}, bf16[192,192]{1,0:T(8,128)(2,1)}, u32[]{:S(2)}) copy-start(bf16[192,192]{1,0:T(8,128)(2,1)} %mix.1) | copy-start | bytes 221188
  3.5 41.2 %copy-start.4 = (f32[768]{0:T(1024)S(1)}, f32[768]{0:T(1024)}, u32[]{:S(2)}) copy-start(f32[768]{0:T(1024)} %dg.1) | copy-start | bytes 9220
  3.5 41.2 %copy-start.5 = (f32[768]{0:T(1024)S(1)}, f32[768]{0:T(1024)}, u32[]{:S(2)}) copy-start(f32[768]{0:T(1024)} %ds.1) | copy-start | bytes 9220
  3.5 41.3 %copy-start.8 = (f32[192]{0:T(256)S(1)}, f32[192]{0:T(256)}, u32[]{:S(2)}) copy-start(f32[192]{0:T(256)} %us.1) | copy-start | bytes 2308

commit v3 on v2

v3 whole, which is shorter than its diff:
```python
import functools

import jax
import jax.numpy as jnp
from jax import lax
from jax.experimental import pallas as pl
from jax.experimental.pallas import tpu as pltpu
from jax.sharding import PartitionSpec as P

MESH = pl.DeviceIdType.MESH
MEMBERS, LEVELS, SLOTS, COLS, C = 2, 8, 34, 6, 192
EXT = SLOTS + 2
HALF = EXT // 2
NZ = 8
ORDER = (4, 3, 5, 2, 6, 1, 7)
ARRIVE = (1, 7, 2, 6, 3, 5, 4)
LAG = 6
BF = jnp.bfloat16
F32 = jnp.float32


def exchange(
    band_hbm, tok_hbm, down_hbm, up_hbm,
    wd, wu, west, east, north, south,
    band_ref, tok, last, own_d, own_u, got_d, got_u, flat_d, flat_u,
    load_sem, s1_send, s1_recv, z_send, z_recv, x_send, x_recv, pair_send, pair_recv,
    col_send, col_recv, row_send, row_recv,
):
    lon, lat, mem = lax.axis_index("lon"), lax.axis_index("lat"), lax.axis_index("mem")
    z, yh = lon // 2, lon % 2
    core, xx = lat % 2, lat // 2
    kind = xx % 2

    loads = [
        pltpu.make_async_copy(down_hbm, own_d, load_sem.at[0]),
        pltpu.make_async_copy(up_hbm, own_u, load_sem.at[1]),
        pltpu.make_async_copy(tok_hbm, tok, load_sem.at[2]),
        pltpu.make_async_copy(band_hbm, band_ref, load_sem.at[3]),
    ]
    for load in loads:
        load.start()

    lon_w, lon_e = (lon + 15) % 16, (lon + 1) % 16
    lat_n, lat_s = (lat + 7) % 8, (lat + 1) % 8
    lon_o, mem_o = 2 * z + 1 - yh, 1 - mem
    mate = (lon, lat + 1 - 2 * core, mem)
    beside = (lon, 2 * ((xx + 1 + 2 * core) % 4) + core, mem)

    def along(d):
        return (2 * ((z + d) % NZ) + yh, lat, mem)

    barrier = pltpu.get_barrier_semaphore()
    partners = [(lon, (lat + d) % 8, mem) for d in range(1, 8)]
    partners += [(lon_o, (lat + d) % 8, mem_o) for d in range(8)]
    partners += [along(d) for d in range(1, NZ)]
    partners += [
        (lon_w, lat, mem), (lon_e, lat, mem),
        (lon_w, lat_n, mem), (lon_w, lat_s, mem), (lon_e, lat_n, mem), (lon_e, lat_s, mem),
    ]
    for where in partners:
        pl.semaphore_signal(barrier, inc=1, device_id=where, device_id_type=MESH)
    for load in loads:
        load.wait()
    live = band_ref[0, 1] - band_ref[0, 0]
    last[...] = tok[:, pl.ds(jnp.clip(live - 1, 0, SLOTS - 1), 1)].reshape(MEMBERS, COLS, LEVELS, C)
    pl.semaphore_wait(barrier, len(partners))

    def copy(src, dst, ssem, rsem, where):
        return pltpu.make_async_remote_copy(
            src_ref=src, dst_ref=dst, send_sem=ssem, recv_sem=rsem,
            device_id=where, device_id_type=MESH,
        )

    firsts = []
    for d in range(2):
        for what, (src, got) in enumerate(((own_d, got_d), (own_u, got_u))):
            lat_t = 2 * ((2 * d + what + 2 * (xx // 2)) % 4) + yh
            i = 4 * d + 2 * what
            firsts.append((lat_t != lat, copy(src, got.at[lat], s1_send.at[i], s1_recv.at[lat], (lon, lat_t, mem))))
            firsts.append((None, copy(src, got.at[lat], s1_send.at[i + 1], s1_recv.at[lat], (lon_o, lat_t, mem_o))))

    def each(op):
        for when, cp in firsts:
            if when is None:
                op(cp)
            else:
                @pl.when(when)
                def _():
                    op(cp)

    each(lambda cp: cp.start())

    to_next = [
        copy(last, north.at[:, 1 : COLS + 1], row_send.at[0], row_recv.at[0], (lon, lat_s, mem)),
        copy(last.at[:, 0], north.at[:, COLS + 1], row_send.at[1], row_recv.at[1], (lon_w, lat_s, mem)),
        copy(last.at[:, COLS - 1], north.at[:, 0], row_send.at[2], row_recv.at[2], (lon_e, lat_s, mem)),
    ]
    to_prev = [
        copy(tok.at[:, 0], south.at[:, 1 : COLS + 1], row_send.at[3], row_recv.at[3], (lon, lat_n, mem)),
        copy(tok.at[:, 0, 0], south.at[:, COLS + 1], row_send.at[4], row_recv.at[4], (lon_w, lat_n, mem)),
        copy(tok.at[:, 0, COLS - 1], south.at[:, 0], row_send.at[5], row_recv.at[5], (lon_e, lat_n, mem)),
    ]

    @pl.when(lat < 7)
    def _():
        for cp in to_next:
            cp.start()

    @pl.when(lat > 0)
    def _():
        for cp in to_prev:
            cp.start()

    @pl.when(lat == 7)
    def _():
        south[...] = jnp.zeros_like(south)

    @pl.when(lat == 0)
    def _():
        north[...] = jnp.zeros_like(north)

    cols = [
        copy(tok.at[:, :, 0], east, col_send.at[0], col_recv.at[0], (lon_w, lat, mem)),
        copy(tok.at[:, :, COLS - 1], west, col_send.at[1], col_recv.at[1], (lon_e, lat, mem)),
    ]

    def gather(own, got, flat, full, rows, other, rows_o):
        span, span_o = 8 * rows, 8 * rows_o
        home = yh == core

        @pl.when(home)
        def _():
            got[pl.ds(lat, 1)] = own[...].reshape(1, *own.shape)

        for i in range(8):
            @pl.when(jnp.logical_not(jnp.logical_and(home, lat == i)))
            def _():
                copy(own, got.at[i], s1_send.at[0], s1_recv.at[i], mate).wait_recv()

        for i in range(8):
            flat[rows * i : rows * (i + 1), :] = got[i].astype(F32)

        def mine(b):
            return full.at[b, pl.ds(pl.multiple_of(core * span, 8), span)]

        def theirs(b):
            return full.at[b, pl.ds(pl.multiple_of((1 - core) * span, 8), span)]

        def cross(b):
            return other.at[b, pl.ds(pl.multiple_of(core * span_o, 8), span_o)]

        def cross_theirs(b):
            return other.at[b, pl.ds(pl.multiple_of((1 - core) * span_o, 8), span_o)]

        full[pl.ds(z, 1), pl.ds(pl.multiple_of(core * span, 8), span), :] = flat[...].astype(BF).reshape(1, *flat.shape)
        order = (0,) + ORDER
        z_out = [copy(mine(z), mine(z), z_send.at[d], z_recv.at[d], along(d)) for d in ORDER]
        for cp in z_out:
            cp.start()
        for cp in cols:
            cp.start()
        started = []

        def pass_on(d):
            b = (z + NZ - d) % NZ
            if d:
                copy(mine(b), mine(b), z_send.at[d], z_recv.at[d], mate).wait_recv()
            for cp in (
                copy(mine(b), mine(b), x_send.at[d], x_recv.at[d], beside),
                copy(mine(b), mine(b), pair_send.at[0, d], pair_recv.at[0, d], mate),
            ):
                cp.start()
                started.append(cp)

        def hand_over(d):
            b = (z + NZ - d) % NZ
            copy(cross(b), cross(b), x_send.at[d], x_recv.at[d], beside).wait_recv()
            cp = copy(cross(b), cross(b), pair_send.at[1, d], pair_recv.at[1, d], mate)
            cp.start()
            started.append(cp)

        arrivals = (0,) + ARRIVE
        for i, d in enumerate(arrivals):
            pass_on(d)
            if i >= LAG:
                hand_over(arrivals[i - LAG])
        for d in arrivals[NZ - LAG :]:
            hand_over(d)
        for d in arrivals:
            b = (z + NZ - d) % NZ
            copy(theirs(b), theirs(b), pair_send.at[0, d], pair_recv.at[0, d], mate).wait_recv()
            copy(cross_theirs(b), cross_theirs(b), pair_send.at[1, d], pair_recv.at[1, d], mate).wait_recv()
        for cp in z_out + started:
            cp.wait_send()

    @pl.when(kind == 0)
    def _():
        gather(own_d, got_d, flat_d, wd, 6, wu, 3)

    @pl.when(kind == 1)
    def _():
        gather(own_u, got_u, flat_u, wu, 3, wd, 6)

    each(lambda cp: cp.wait_send())
    for cp in cols:
        cp.wait()

    @pl.when(lat < 7)
    def _():
        for cp in to_next:
            cp.wait_send()
        for cp in to_prev:
            cp.wait_recv()

    @pl.when(lat > 0)
    def _():
        for cp in to_prev:
            cp.wait_send()
        for cp in to_next:
            cp.wait_recv()


def run_exchange(band_rows, tok, down, up):
    dma = pltpu.SemaphoreType.DMA
    vmem = pl.BlockSpec(memory_space=pltpu.VMEM)
    hbm = pl.BlockSpec(memory_space=pltpu.HBM)
    col = (MEMBERS, SLOTS, LEVELS, C)
    row = (MEMBERS, COLS + 2, LEVELS, C)
    return pl.pallas_call(
        exchange,
        out_shape=[
            jax.ShapeDtypeStruct((NZ, 96, 384), BF),
            jax.ShapeDtypeStruct((NZ, 48, 768), BF),
            jax.ShapeDtypeStruct(col, BF),
            jax.ShapeDtypeStruct(col, BF),
            jax.ShapeDtypeStruct(row, BF),
            jax.ShapeDtypeStruct(row, BF),
        ],
        in_specs=[hbm] * 4,
        out_specs=[vmem] * 6,
        scratch_shapes=[
            pltpu.SMEM((1, 2), jnp.int32),
            pltpu.VMEM((MEMBERS, SLOTS, COLS, LEVELS, C), BF),
            pltpu.VMEM((MEMBERS, COLS, LEVELS, C), BF),
            pltpu.VMEM((6, 384), BF),
            pltpu.VMEM((3, 768), BF),
            pltpu.VMEM((8, 6, 384), BF),
            pltpu.VMEM((8, 3, 768), BF),
            pltpu.VMEM((48, 384), F32),
            pltpu.VMEM((24, 768), F32),
            dma((4,)), dma((8,)), dma((8,)), dma((NZ,)), dma((NZ,)), dma((NZ,)), dma((NZ,)),
            dma((2, NZ)), dma((2, NZ)), dma((2,)), dma((2,)), dma((6,)), dma((6,)),
        ],
        compiler_params=pltpu.CompilerParams(
            collective_id=0, has_side_effects=True, vmem_limit_bytes=24 << 20
        ),
        name="exchange",
    )(*(pltpu.with_memory_space_constraint(v, pltpu.HBM) for v in (band_rows, tok, down, up)))


GROUP = 6


def patches(
    band_ref, tok, wd, wu, west, east, north, south, dg, ds, ug, us, mix_hbm,
    out_hbm, mix, ext, fine, wu4, load_sem, store_sem,
):
    lat = lax.axis_index("lat")
    shift = jnp.minimum(lat, 1)
    live = band_ref[0, 1] - band_ref[0, 0]
    load = pltpu.make_async_copy(mix_hbm, mix, load_sem)
    load.start()
    for g in range(4):
        wu4[g] = wu[:, C * g : C * (g + 1)]
    ext[:, pl.ds(shift, SLOTS), 0] = west[...]
    ext[:, pl.ds(shift, SLOTS), COLS + 1] = east[...]
    ext[:, pl.ds(shift, SLOTS), 1 : COLS + 1] = tok[...]

    @pl.when(lat > 0)
    def _():
        ext[:, 0] = north[...]

    ext[:, pl.ds(jnp.clip(live + shift, 0, EXT - 1), 1)] = south[...].reshape(MEMBERS, 1, COLS + 2, LEVELS, C)

    load.wait()
    view = ext.reshape(MEMBERS, HALF, 2, 4, 2, LEVELS, C)
    eps = 1e-05
    gains, shifts = dg[...].reshape(1, 4 * C), ds[...].reshape(1, 4 * C)
    fine_gain, fine_shift = ug[...].reshape(1, C), us[...].reshape(1, C)
    stores = []
    for m in range(MEMBERS):
        @pl.loop(0, HALF // GROUP)
        def _(it):
            k0 = it * GROUP
            cells = {}
            total = None
            for q in range(2):
                for p in range(2):
                    x = jnp.concatenate(
                        [view[m, pl.ds(k0, GROUP), p, j, q].reshape(GROUP * LEVELS, C) for j in range(4)], axis=0
                    ).astype(F32)
                    cells[q, p] = x
                    s = jnp.sum(x, axis=1, keepdims=True)
                    total = s if total is None else total + s
            average = total * (1.0 / (4 * C))
            total = None
            for key in cells:
                cells[key] = cells[key] - average
                s = jnp.sum(cells[key] * cells[key], axis=1, keepdims=True)
                total = s if total is None else total + s
            scale = lax.rsqrt(total * (1.0 / (4 * C)) + eps)
            coarse = None
            for q in range(2):
                for p in range(2):
                    g = 2 * q + p
                    normed = (cells[q, p] * scale * gains[:, C * g : C * (g + 1)] + shifts[:, C * g : C * (g + 1)]).astype(BF)
                    term = jnp.dot(normed, wd[C * g : C * (g + 1), :], preferred_element_type=F32)
                    coarse = term if coarse is None else coarse + term
            coarse = coarse.astype(BF)
            n = GROUP * LEVELS
            for p in range(2):
                for q in range(2):
                    j0 = 1 - q
                    grown = jnp.dot(coarse[n * j0 : n * (j0 + 3)], wu4[2 * p + q], preferred_element_type=F32)
                    average = jnp.sum(grown, axis=1, keepdims=True) * (1.0 / C)
                    grown = grown - average
                    spread = jnp.sum(grown * grown, axis=1, keepdims=True) * (1.0 / C)
                    normed = (grown * lax.rsqrt(spread + eps) * fine_gain + fine_shift).astype(BF)
                    done = jnp.dot(normed, mix[...], preferred_element_type=F32).astype(BF)
                    done = done.reshape(3, GROUP, LEVELS, C)
                    rows = 2 * (k0 + lax.broadcasted_iota(jnp.int32, (GROUP, LEVELS, C), 0)) + p
                    keep = rows < live + shift
                    for j in range(3):
                        fine[m, pl.ds(k0, GROUP), p, 2 * (j + j0) + q - 1] = jnp.where(keep, done[j], jnp.zeros_like(done[j]))
        rows_out = fine.reshape(MEMBERS, EXT, COLS, LEVELS, C)
        store = pltpu.make_async_copy(rows_out.at[m, pl.ds(shift, SLOTS)], out_hbm.at[m], store_sem.at[m])
        store.start()
        stores.append(store)
    for store in stores:
        store.wait()


def run_patches(band_rows, tok, wd, wu, west, east, north, south, dg, ds, ug, us, mix):
    vmem = pl.BlockSpec(memory_space=pltpu.VMEM)
    anywhere = pl.BlockSpec(memory_space=pl.ANY)
    return pl.pallas_call(
        patches,
        out_shape=jax.ShapeDtypeStruct((MEMBERS, SLOTS, COLS, LEVELS, C), BF),
        in_specs=[pl.BlockSpec(memory_space=pltpu.SMEM), vmem] + [vmem] * 10 + [pl.BlockSpec(memory_space=pltpu.HBM)],
        out_specs=anywhere,
        scratch_shapes=[
            pltpu.VMEM((C, C), BF),
            pltpu.VMEM((MEMBERS, EXT, COLS + 2, LEVELS, C), BF),
            pltpu.VMEM((MEMBERS, HALF, 2, COLS, LEVELS, C), BF),
            pltpu.VMEM((4, 2 * C, C), BF),
            pltpu.SemaphoreType.DMA,
            pltpu.SemaphoreType.DMA((MEMBERS,)),
        ],
        compiler_params=pltpu.CompilerParams(vmem_limit_bytes=24 << 20),
        name="patches",
    )(band_rows, tok, wd, wu, west, east, north, south, dg, ds, ug, us, pltpu.with_memory_space_constraint(mix, pltpu.HBM))


def body(
    tokens, band_rows, down_gain, down_shift, down_weight, up_weight, up_gain, up_shift, mix_weight
):
    tok = tokens.transpose(0, 2, 3, 1, 4)
    wd, wu, west, east, north, south = run_exchange(band_rows, tok, down_weight, up_weight)
    out = run_patches(
        band_rows, tok, wd.reshape(4 * C, 2 * C), wu.reshape(2 * C, 4 * C), west, east, north, south,
        down_gain, down_shift, up_gain, up_shift, mix_weight,
    )
    return out.transpose(0, 3, 1, 2, 4)


def solution(mesh):
    return jax.shard_map(
        body,
        mesh=mesh,
        in_specs=(
            P("mem", None, "lat", "lon", None),
            P("lat", None),
            P(),
            P(),
            P(("lon", "lat"), None),
            P(("lon", "lat"), None),
            P(),
            P(),
            P(),
        ),
        out_specs=P("mem", None, "lat", "lon", None),
        check_vma=False,
    )
```

time: 60 us -> 46.8 us (0.78)
  the two profiles are of different devices: /device:TPU:3 before, /device:TPU:1 now
where the time goes in v3:
time: 46.8 us; the launch traced here: 46.7 us
  Pallas kernels  46.6 us (100%)
    pallas_call x1, Pallas kernels, run_exchange(): pl.pallas_call(exchange, out_shape=[jax.ShapeDtypeStruct((NZ, 96, 384), B...  31 us
    pallas_call x1, Pallas kernels, run_patches(): pl.pallas_call(patches, out_shape=jax.ShapeDtypeStruct((MEMBERS, SLOTS, C...  15.6 us

profile of v3, /device:TPU:1, one launch (start us, length us, event | category | flops | bytes accessed | tf_op | source)
XLA Modules:
  0.0 46.7 jit_solution(16039764272952397317)
XLA Ops:
  0.0 0.0 copy-start.3
  0.0 0.0 copy-start.5
  0.0 0.0 copy-start.4
  0.0 0.0 copy-start.2
  0.0 0.0 copy-start.1
  0.0 0.0 copy-start
  0.0 31.0 %exchange.1 = (bf16[8,96,384]{2,1,0:T(8,128)(2,1)S(1)}, bf16[8,48,768]{2,1,0:T(8,128)(2,1)S(1)}, bf16[2,34,8,192]{3,2,1,0:T(8,128)(2,1)S(1)}, bf16[2,34,8,192]{3...) custom-call(s32[1,2]{1,0:T(1,128)} %band_ref.1, ...), custom_call_target="tpu_custom_call" | custom-call | tf_op jit(solution)/shard_map/exchange/pallas_call | solution.py:229
  31.0 0.0 copy-done.3
  31.0 0.0 copy-done.5
  31.0 0.0 copy-done.4
  31.0 0.0 copy-done.2
  31.0 0.0 copy-done.1
  31.1 0.0 copy-done
  31.1 15.6 %patches.1 = bf16[2,34,6,8,192]{4,3,2,1,0:T(8,128)(2,1)} custom-call(s32[1,2]{1,0:T(1,128)S(1)} %copy-done.3, bf16[2,34,6,8,192]{4,3,2,1,0:T(8,128)(2,1)S(1)} %bitcast.5, bf16[768,384]{1,0:T(8,128)(2,1)S(1)} %bitcast.6, bf16[384,768]{1,0:T(8,128)(2,1)S(1)} %bitcast.7, bf16[2,34,8,192]{3,2,1,0:T(8,128)(2,1)S(1)} %get-tuple-element.13.west, ...), custom_call_target="tpu_custom_call" | custom-call | tf_op jit(solution)/shard_map/patches/pallas_call | solution.py:346
Async XLA Ops:
  0.0 31.0 %copy-start.3 = (s32[1,2]{1,0:T(1,128)S(1)}, s32[1,2]{1,0:T(1,128)}, u32[]{:S(2)}) copy-start(s32[1,2]{1,0:T(1,128)} %band_ref.1) | copy-start | bytes 28
  0.0 31.0 %copy-start.5 = (f32[192]{0:T(256)S(1)}, f32[192]{0:T(256)}, u32[]{:S(2)}) copy-start(f32[192]{0:T(256)} %us.1) | copy-start | bytes 2308
  0.0 31.0 %copy-start.4 = (f32[192]{0:T(256)S(1)}, f32[192]{0:T(256)}, u32[]{:S(2)}) copy-start(f32[192]{0:T(256)} %ug.1) | copy-start | bytes 2308
  0.0 31.0 %copy-start.2 = (f32[768]{0:T(1024)S(1)}, f32[768]{0:T(1024)}, u32[]{:S(2)}) copy-start(f32[768]{0:T(1024)} %ds.1) | copy-start | bytes 9220
  0.0 31.0 %copy-start.1 = (f32[768]{0:T(1024)S(1)}, f32[768]{0:T(1024)}, u32[]{:S(2)}) copy-start(f32[768]{0:T(1024)} %dg.1) | copy-start | bytes 9220
  0.0 31.0 %copy-start = (bf16[2,8,34,6,192]{4,1,3,2,0:T(8,128)(2,1)S(1)}, bf16[2,8,34,6,192]{4,1,3,2,0:T(8,128)(2,1)}, u32[]{:S(2)}) copy-start(bf16[2,8,34,6,192]{4,1,3,2,0:T(8,128)(2,1)} %param.9) | copy-start | bytes 3760132

commit v4 on v3

v4 whole, which is shorter than its diff:
```python
import functools

import jax
import jax.numpy as jnp
from jax import lax
from jax.experimental import pallas as pl
from jax.experimental.pallas import tpu as pltpu
from jax.sharding import PartitionSpec as P

MESH = pl.DeviceIdType.MESH
MEMBERS, LEVELS, SLOTS, COLS, C = 2, 8, 34, 6, 192
EXT = SLOTS + 2
HALF = EXT // 2
NZ = 8
ORDER = (4, 3, 5, 2, 6, 1, 7)
ARRIVE = (1, 7, 2, 6, 3, 5, 4)
LAG = 6
INSIDE = 0
BF = jnp.bfloat16
F32 = jnp.float32


def exchange(
    band_hbm, tok_hbm, down_hbm, up_hbm, dg_hbm, ds_hbm,
    wd, wu, normed,
    band_ref, dg, ds, tok, west, east, north, south, last, own_d, own_u, got_d, got_u, flat_d, flat_u,
    load_sem, s1_send, s1_recv, z_send, z_recv, x_send, x_recv, pair_send, pair_recv,
    col_send, col_recv, row_send, row_recv,
):
    lon, lat, mem = lax.axis_index("lon"), lax.axis_index("lat"), lax.axis_index("mem")
    z, yh = lon // 2, lon % 2
    core, xx = lat % 2, lat // 2
    kind = xx % 2
    shift = jnp.minimum(lat, 1)

    loads = [
        pltpu.make_async_copy(down_hbm, own_d, load_sem.at[0]),
        pltpu.make_async_copy(up_hbm, own_u, load_sem.at[1]),
        pltpu.make_async_copy(tok_hbm, tok.at[:, pl.ds(shift, SLOTS)], load_sem.at[2]),
        pltpu.make_async_copy(band_hbm, band_ref, load_sem.at[3]),
        pltpu.make_async_copy(dg_hbm, dg, load_sem.at[4]),
        pltpu.make_async_copy(ds_hbm, ds, load_sem.at[5]),
    ]
    for load in loads:
        load.start()

    lon_w, lon_e = (lon + 15) % 16, (lon + 1) % 16
    lat_n, lat_s = (lat + 7) % 8, (lat + 1) % 8
    lon_o, mem_o = 2 * z + 1 - yh, 1 - mem
    mate = (lon, lat + 1 - 2 * core, mem)
    beside = (lon, 2 * ((xx + 1 + 2 * core) % 4) + core, mem)

    def along(d):
        return (2 * ((z + d) % NZ) + yh, lat, mem)

    barrier = pltpu.get_barrier_semaphore()
    partners = [(lon, (lat + d) % 8, mem) for d in range(1, 8)]
    partners += [(lon_o, (lat + d) % 8, mem_o) for d in range(8)]
    partners += [along(d) for d in range(1, NZ)]
    partners += [
        (lon_w, lat, mem), (lon_e, lat, mem),
        (lon_w, lat_n, mem), (lon_w, lat_s, mem), (lon_e, lat_n, mem), (lon_e, lat_s, mem),
    ]
    for where in partners:
        pl.semaphore_signal(barrier, inc=1, device_id=where, device_id_type=MESH)
    for load in loads:
        load.wait()
    live = band_ref[0, 1] - band_ref[0, 0]
    last[...] = tok[:, pl.ds(jnp.clip(live - 1, 0, SLOTS - 1) + shift, 1)].reshape(MEMBERS, COLS, LEVELS, C)
    pl.semaphore_wait(barrier, len(partners))

    def copy(src, dst, ssem, rsem, where):
        return pltpu.make_async_remote_copy(
            src_ref=src, dst_ref=dst, send_sem=ssem, recv_sem=rsem,
            device_id=where, device_id_type=MESH,
        )

    firsts = []
    for d in range(2):
        for what, (src, got) in enumerate(((own_d, got_d), (own_u, got_u))):
            lat_t = 2 * ((2 * d + what + 2 * (xx // 2)) % 4) + yh
            i = 4 * d + 2 * what
            firsts.append((lat_t != lat, copy(src, got.at[lat], s1_send.at[i], s1_recv.at[lat], (lon, lat_t, mem))))
            firsts.append((None, copy(src, got.at[lat], s1_send.at[i + 1], s1_recv.at[lat], (lon_o, lat_t, mem_o))))

    def each(op):
        for when, cp in firsts:
            if when is None:
                op(cp)
            else:
                @pl.when(when)
                def _():
                    op(cp)

    each(lambda cp: cp.start())

    to_next = [
        copy(last, north.at[:, 1 : COLS + 1], row_send.at[0], row_recv.at[0], (lon, lat_s, mem)),
        copy(last.at[:, 0], north.at[:, COLS + 1], row_send.at[1], row_recv.at[1], (lon_w, lat_s, mem)),
        copy(last.at[:, COLS - 1], north.at[:, 0], row_send.at[2], row_recv.at[2], (lon_e, lat_s, mem)),
    ]
    to_prev = [
        copy(tok.at[:, shift], south.at[:, 1 : COLS + 1], row_send.at[3], row_recv.at[3], (lon, lat_n, mem)),
        copy(tok.at[:, shift, 0], south.at[:, COLS + 1], row_send.at[4], row_recv.at[4], (lon_w, lat_n, mem)),
        copy(tok.at[:, shift, COLS - 1], south.at[:, 0], row_send.at[5], row_recv.at[5], (lon_e, lat_n, mem)),
    ]

    @pl.when(lat < 7)
    def _():
        for cp in to_next:
            cp.start()

    @pl.when(lat > 0)
    def _():
        for cp in to_prev:
            cp.start()

    @pl.when(lat == 7)
    def _():
        south[...] = jnp.zeros_like(south)

    @pl.when(lat == 0)
    def _():
        north[...] = jnp.zeros_like(north)

    cols = [
        copy(tok.at[:, pl.ds(shift, SLOTS), 0], east.at[:, pl.ds(shift, SLOTS)], col_send.at[0], col_recv.at[0], (lon_w, lat, mem)),
        copy(tok.at[:, pl.ds(shift, SLOTS), COLS - 1], west.at[:, pl.ds(shift, SLOTS)], col_send.at[1], col_recv.at[1], (lon_e, lat, mem)),
    ]

    spot = (live + shift) // 2
    gains, shifts = dg[...].reshape(1, 4 * C), ds[...].reshape(1, 4 * C)

    def cell(m, j, q, p):
        i = 2 * j + q
        if i == 0:
            x = west.reshape(MEMBERS, HALF, 2, LEVELS, C)[m, :, p]
        elif i == COLS + 1:
            x = east.reshape(MEMBERS, HALF, 2, LEVELS, C)[m, :, p]
        else:
            x = tok.reshape(MEMBERS, HALF, 2, COLS, LEVELS, C)[m, :, p, i - 1]
        if p:
            here = lax.broadcasted_iota(jnp.int32, (HALF, LEVELS, C), 0) == spot
            x = jnp.where(here, south[m, i].reshape(1, LEVELS, C), x)
        return x.reshape(HALF * LEVELS, C).astype(F32)

    def norm(j):
        @pl.loop(0, MEMBERS)
        def _(m):
            cells = {(q, p): cell(m, j, q, p) for q in range(2) for p in range(2)}
            total = sum(jnp.sum(x, axis=1, keepdims=True) for x in cells.values())
            average = total * (1.0 / (4 * C))
            cells = {key: x - average for key, x in cells.items()}
            total = sum(jnp.sum(x * x, axis=1, keepdims=True) for x in cells.values())
            scale = lax.rsqrt(total * (1.0 / (4 * C)) + 1e-05)
            for (q, p), x in cells.items():
                g = 2 * q + p
                y = x * scale * gains[:, C * g : C * (g + 1)] + shifts[:, C * g : C * (g + 1)]
                normed[g, j, m] = y.astype(BF)

    def inside():
        @pl.when(lat < 7)
        def _():
            for cp in to_prev:
                cp.wait_recv()

        @pl.when(lat > 0)
        def _():
            for cp in to_next:
                cp.wait_recv()
            tok[:, 0] = north[:, 1 : COLS + 1]

        norm(1)
        norm(2)

    def border():
        for cp in cols:
            cp.wait_recv()

        @pl.when(lat > 0)
        def _():
            west[:, 0] = north[:, 0]
            east[:, 0] = north[:, COLS + 1]

        norm(0)
        norm(3)

    def gather(own, got, flat, full, rows, other, rows_o):
        span, span_o = 8 * rows, 8 * rows_o
        home = yh == core

        @pl.when(home)
        def _():
            got[pl.ds(lat, 1)] = own[...].reshape(1, *own.shape)

        for i in range(8):
            @pl.when(jnp.logical_not(jnp.logical_and(home, lat == i)))
            def _():
                copy(own, got.at[i], s1_send.at[0], s1_recv.at[i], mate).wait_recv()

        for i in range(8):
            flat[rows * i : rows * (i + 1), :] = got[i].astype(F32)

        def mine(b):
            return full.at[b, pl.ds(pl.multiple_of(core * span, 8), span)]

        def theirs(b):
            return full.at[b, pl.ds(pl.multiple_of((1 - core) * span, 8), span)]

        def cross(b):
            return other.at[b, pl.ds(pl.multiple_of(core * span_o, 8), span_o)]

        def cross_theirs(b):
            return other.at[b, pl.ds(pl.multiple_of((1 - core) * span_o, 8), span_o)]

        full[pl.ds(z, 1), pl.ds(pl.multiple_of(core * span, 8), span), :] = flat[...].astype(BF).reshape(1, *flat.shape)
        order = (0,) + ORDER
        z_out = [copy(mine(z), mine(z), z_send.at[d], z_recv.at[d], along(d)) for d in ORDER]
        for cp in z_out:
            cp.start()
        for cp in cols:
            cp.start()
        started = []

        def pass_on(d):
            b = (z + NZ - d) % NZ
            if d:
                copy(mine(b), mine(b), z_send.at[d], z_recv.at[d], mate).wait_recv()
            for cp in (
                copy(mine(b), mine(b), x_send.at[d], x_recv.at[d], beside),
                copy(mine(b), mine(b), pair_send.at[0, d], pair_recv.at[0, d], mate),
            ):
                cp.start()
                started.append(cp)

        def hand_over(d):
            b = (z + NZ - d) % NZ
            copy(cross(b), cross(b), x_send.at[d], x_recv.at[d], beside).wait_recv()
            cp = copy(cross(b), cross(b), pair_send.at[1, d], pair_recv.at[1, d], mate)
            cp.start()
            started.append(cp)

        arrivals = (0,) + ARRIVE
        for i, d in enumerate(arrivals):
            pass_on(d)
            if i == INSIDE:
                inside()
            if i >= LAG:
                hand_over(arrivals[i - LAG])
        for d in arrivals[NZ - LAG :]:
            hand_over(d)
        border()
        for d in arrivals:
            b = (z + NZ - d) % NZ
            copy(theirs(b), theirs(b), pair_send.at[0, d], pair_recv.at[0, d], mate).wait_recv()
            copy(cross_theirs(b), cross_theirs(b), pair_send.at[1, d], pair_recv.at[1, d], mate).wait_recv()
        for cp in z_out + started:
            cp.wait_send()

    @pl.when(kind == 0)
    def _():
        gather(own_d, got_d, flat_d, wd, 6, wu, 3)

    @pl.when(kind == 1)
    def _():
        gather(own_u, got_u, flat_u, wu, 3, wd, 6)

    each(lambda cp: cp.wait_send())
    for cp in cols:
        cp.wait_send()

    @pl.when(lat < 7)
    def _():
        for cp in to_next:
            cp.wait_send()

    @pl.when(lat > 0)
    def _():
        for cp in to_prev:
            cp.wait_send()


def run_exchange(band_rows, tok, down, up, dg, ds):
    dma = pltpu.SemaphoreType.DMA
    vmem = pl.BlockSpec(memory_space=pltpu.VMEM)
    hbm = pl.BlockSpec(memory_space=pltpu.HBM)
    col = (MEMBERS, EXT, LEVELS, C)
    row = (MEMBERS, COLS + 2, LEVELS, C)
    return pl.pallas_call(
        exchange,
        out_shape=[
            jax.ShapeDtypeStruct((NZ, 96, 384), BF),
            jax.ShapeDtypeStruct((NZ, 48, 768), BF),
            jax.ShapeDtypeStruct((4, 4, MEMBERS, HALF * LEVELS, C), BF),
        ],
        in_specs=[hbm] * 6,
        out_specs=[vmem] * 3,
        scratch_shapes=[
            pltpu.SMEM((1, 2), jnp.int32),
            pltpu.VMEM((4 * C,), F32),
            pltpu.VMEM((4 * C,), F32),
            pltpu.VMEM((MEMBERS, EXT, COLS, LEVELS, C), BF),
            pltpu.VMEM(col, BF),
            pltpu.VMEM(col, BF),
            pltpu.VMEM(row, BF),
            pltpu.VMEM(row, BF),
            pltpu.VMEM((MEMBERS, COLS, LEVELS, C), BF),
            pltpu.VMEM((6, 384), BF),
            pltpu.VMEM((3, 768), BF),
            pltpu.VMEM((8, 6, 384), BF),
            pltpu.VMEM((8, 3, 768), BF),
            pltpu.VMEM((48, 384), F32),
            pltpu.VMEM((24, 768), F32),
            dma((6,)), dma((8,)), dma((8,)), dma((NZ,)), dma((NZ,)), dma((NZ,)), dma((NZ,)),
            dma((2, NZ)), dma((2, NZ)), dma((2,)), dma((2,)), dma((6,)), dma((6,)),
        ],
        compiler_params=pltpu.CompilerParams(
            collective_id=0, has_side_effects=True, vmem_limit_bytes=24 << 20
        ),
        name="exchange",
    )(*(pltpu.with_memory_space_constraint(v, pltpu.HBM) for v in (band_rows, tok, down, up, dg, ds)))


SPLIT = ((0, 1),)
ROWS = HALF * LEVELS


def patches(
    band_hbm, wd, wu, normed, ug, us, mix_hbm,
    out_hbm, band_ref, mix, fine, wu4, load_sem, store_sem,
):
    lat = lax.axis_index("lat")
    shift = jnp.minimum(lat, 1)
    loads = [
        pltpu.make_async_copy(mix_hbm, mix, load_sem.at[0]),
        pltpu.make_async_copy(band_hbm, band_ref, load_sem.at[1]),
    ]
    for load in loads:
        load.start()
    for g in range(4):
        wu4[g] = wu[:, C * g : C * (g + 1)]
    eps = 1e-05
    fine_gain, fine_shift = ug[...].reshape(1, C), us[...].reshape(1, C)
    rows_out = fine.reshape(MEMBERS, EXT, COLS, LEVELS, C)
    stores = []
    for members in SPLIT:
        def pick(g):
            return jnp.concatenate([normed[g, j, m] for j in range(4) for m in members], axis=0)

        coarse = None
        for g in range(4):
            term = jnp.dot(pick(g), wd[C * g : C * (g + 1), :], preferred_element_type=F32)
            coarse = term if coarse is None else coarse + term
        coarse = coarse.astype(BF)
        if members == SPLIT[0]:
            for load in loads:
                load.wait()
            bound = band_ref[0, 1] - band_ref[0, 0] + shift
        n = ROWS * len(members)
        for p in range(2):
            keep = 2 * lax.broadcasted_iota(jnp.int32, (HALF, LEVELS, C), 0) + p < bound
            for q in range(2):
                j0 = 1 - q
                grown = jnp.dot(coarse[n * j0 : n * (j0 + 3)], wu4[2 * p + q], preferred_element_type=F32)
                average = jnp.sum(grown, axis=1, keepdims=True) * (1.0 / C)
                grown = grown - average
                spread = jnp.sum(grown * grown, axis=1, keepdims=True) * (1.0 / C)
                unit = (grown * lax.rsqrt(spread + eps) * fine_gain + fine_shift).astype(BF)
                done = jnp.dot(unit, mix[...], preferred_element_type=F32).astype(BF)
                done = done.reshape(3, len(members), HALF, LEVELS, C)
                for j in range(3):
                    for i, m in enumerate(members):
                        fine[m, :, p, 2 * (j + j0) + q - 1] = jnp.where(keep, done[j, i], jnp.zeros_like(done[j, i]))
        for m in members:
            store = pltpu.make_async_copy(rows_out.at[m, pl.ds(shift, SLOTS)], out_hbm.at[m], store_sem.at[m])
            store.start()
            stores.append(store)
    for store in stores:
        store.wait()


def run_patches(band_rows, wd, wu, normed, ug, us, mix):
    vmem = pl.BlockSpec(memory_space=pltpu.VMEM)
    hbm = pl.BlockSpec(memory_space=pltpu.HBM)
    band_rows, mix = (pltpu.with_memory_space_constraint(v, pltpu.HBM) for v in (band_rows, mix))
    return pl.pallas_call(
        patches,
        out_shape=jax.ShapeDtypeStruct((MEMBERS, SLOTS, COLS, LEVELS, C), BF),
        in_specs=[hbm] + [vmem] * 5 + [hbm],
        out_specs=pl.BlockSpec(memory_space=pl.ANY),
        scratch_shapes=[
            pltpu.SMEM((1, 2), jnp.int32),
            pltpu.VMEM((C, C), BF),
            pltpu.VMEM((MEMBERS, HALF, 2, COLS, LEVELS, C), BF),
            pltpu.VMEM((4, 2 * C, C), BF),
            pltpu.SemaphoreType.DMA((2,)),
            pltpu.SemaphoreType.DMA((MEMBERS,)),
        ],
        compiler_params=pltpu.CompilerParams(vmem_limit_bytes=24 << 20),
        name="patches",
    )(band_rows, wd, wu, normed, ug, us, mix)


def body(
    tokens, band_rows, down_gain, down_shift, down_weight, up_weight, up_gain, up_shift, mix_weight
):
    tok = tokens.transpose(0, 2, 3, 1, 4)
    wd, wu, normed = run_exchange(band_rows, tok, down_weight, up_weight, down_gain, down_shift)
    out = run_patches(
        band_rows, wd.reshape(4 * C, 2 * C), wu.reshape(2 * C, 4 * C), normed, up_gain, up_shift, mix_weight
    )
    return out.transpose(0, 3, 1, 2, 4)


def solution(mesh):
    return jax.shard_map(
        body,
        mesh=mesh,
        in_specs=(
            P("mem", None, "lat", "lon", None),
            P("lat", None),
            P(),
            P(),
            P(("lon", "lat"), None),
            P(("lon", "lat"), None),
            P(),
            P(),
            P(),
        ),
        out_specs=P("mem", None, "lat", "lon", None),
        check_vma=False,
    )
```

time: 46.8 us -> 38.8 us (0.83)
  Pallas kernels: 46.6 us -> 38.7 us
    pallas_call x1, Pallas kernels: 15.6 us -> 6.88 us  [run_patches(): pl.pallas_call(patches, out_shape=jax.ShapeDtypeStruct((MEMBERS, SLOTS, C...]
    pallas_call x1, Pallas kernels: 31 us -> 31.8 us  [run_exchange(): pl.pallas_call(exchange, out_shape=[jax.ShapeDtypeStruct((NZ, 96, 384), B...]
where the time goes in v4:
time: 38.8 us; the launch traced here: 38.7 us
  Pallas kernels  38.7 us (100%)
    pallas_call x1, Pallas kernels, run_exchange(): pl.pallas_call(exchange, out_shape=[jax.ShapeDtypeStruct((NZ, 96, 384), B...  31.8 us
    pallas_call x1, Pallas kernels, run_patches(): pl.pallas_call(patches, out_shape=jax.ShapeDtypeStruct((MEMBERS, SLOTS, C...  6.88 us

profile of v4, /device:TPU:1, one launch (start us, length us, event | category | flops | bytes accessed | tf_op | source)
XLA Modules:
  0.0 38.7 jit_solution(3662929341809380907)
XLA Ops:
  0.0 0.0 copy-start.1
  0.0 0.0 copy-start
  0.0 31.8 %exchange.1 = (bf16[8,96,384]{2,1,0:T(8,128)(2,1)S(1)}, bf16[8,48,768]{2,1,0:T(8,128)(2,1)S(1)}, bf16[4,4,2,144,192]{4,3,2,1,0:T(8,128)(2,1)S(1)}) custom-call(s32[1,2]{1,0:T(1,128)} %band_hbm.3, bf16[2,34,6,8,192]{4,3,2,1,0:T(8,128)(2,1)} %bitcast.6, bf16[6,384]{1,0:T(8,128)(2,1)} %down_hbm.1, bf16[3,768]{1,0:T(4,128)(2,1)} %up_hbm.1, f32[768]{0:T(1024)} %dg_hbm.1, ...), custom_call_target="tpu_custom_call" | custom-call | tf_op jit(solution)/shard_map/exchange/pallas_call | solution.py:289
  31.8 0.0 copy-done.1
  31.8 0.0 copy-done
  31.9 6.9 %patches.1 = bf16[2,34,6,8,192]{4,3,2,1,0:T(8,128)(2,1)} custom-call(s32[1,2]{1,0:T(1,128)} %band_hbm.3, bf16[768,384]{1,0:T(8,128)(2,1)S(1)} %bitcast.4, bf16[384,768]{1,0:T(8,128)(2,1)S(1)} %bitcast.5, bf16[4,4,2,144,192]{4,3,2,1,0:T(8,128)(2,1)S(1)} %get-tuple-element.10.normed, f32[192]{0:T(256)S(1)} %copy-done, f32[192]{0:T(256)S(1)} %copy-done.1, ...), custom_call_target="tpu_custom_call" | custom-call | tf_op jit(solution)/shard_map/patches/pallas_call | solution.py:386
Async XLA Ops:
  0.0 31.8 %copy-start.1 = (f32[192]{0:T(256)S(1)}, f32[192]{0:T(256)}, u32[]{:S(2)}) copy-start(f32[192]{0:T(256)} %us.1) | copy-start | bytes 2308
  0.0 31.8 %copy-start = (f32[192]{0:T(256)S(1)}, f32[192]{0:T(256)}, u32[]{:S(2)}) copy-start(f32[192]{0:T(256)} %ug.1) | copy-start | bytes 2308

commit v5 on v4

--- a/solution.py
+++ b/solution.py
@@ -12,10 +12,12 @@
 EXT = SLOTS + 2
 HALF = EXT // 2
 NZ = 8
-ORDER = (4, 3, 5, 2, 6, 1, 7)
+ORDER = (1, 7, 2, 6, 3, 5, 4)
 ARRIVE = (1, 7, 2, 6, 3, 5, 4)
 LAG = 6
 INSIDE = 0
+COLS_AT = (-1, -1)
+MIX = 0
 BF = jnp.bfloat16
 F32 = jnp.float32
 
@@ -23,14 +25,15 @@
 def exchange(
     band_hbm, tok_hbm, down_hbm, up_hbm, dg_hbm, ds_hbm,
     wd, wu, normed,
-    band_ref, dg, ds, tok, west, east, north, south, last, own_d, own_u, got_d, got_u, flat_d, flat_u,
+    band_ref, dg, ds, tok, first_col, last_col, west, east, north, south, last, own_d, own_u, got_d, got_u, flat,
     load_sem, s1_send, s1_recv, z_send, z_recv, x_send, x_recv, pair_send, pair_recv,
     col_send, col_recv, row_send, row_recv,
 ):
     lon, lat, mem = lax.axis_index("lon"), lax.axis_index("lat"), lax.axis_index("mem")
     z, yh = lon // 2, lon % 2
     core, xx = lat % 2, lat // 2
-    kind = xx % 2
+    quarter = (xx + 2 * mem * MIX) % 4
+    cy, ch = quarter % 2, quarter // 2
     shift = jnp.minimum(lat, 1)
 
     loads = [
@@ -44,29 +47,39 @@
     for load in loads:
         load.start()
 
+    @pl.when(lat > 0)
+    def _():
+        tok[:, 0] = jnp.zeros((MEMBERS, COLS, LEVELS, C), BF)
+        tok[:, EXT - 1] = jnp.zeros((MEMBERS, COLS, LEVELS, C), BF)
+
+    @pl.when(lat == 0)
+    def _():
+        tok[:, SLOTS:] = jnp.zeros((MEMBERS, 2, COLS, LEVELS, C), BF)
+
     lon_w, lon_e = (lon + 15) % 16, (lon + 1) % 16
     lat_n, lat_s = (lat + 7) % 8, (lat + 1) % 8
     lon_o, mem_o = 2 * z + 1 - yh, 1 - mem
     mate = (lon, lat + 1 - 2 * core, mem)
-    beside = (lon, 2 * ((xx + 1 + 2 * core) % 4) + core, mem)
 
     def along(d):
         return (2 * ((z + d) % NZ) + yh, lat, mem)
+
+    def across(s):
+        return (lon, (lat + 2 * s) % 8, mem)
 
     barrier = pltpu.get_barrier_semaphore()
     partners = [(lon, (lat + d) % 8, mem) for d in range(1, 8)]
     partners += [(lon_o, (lat + d) % 8, mem_o) for d in range(8)]
     partners += [along(d) for d in range(1, NZ)]
+    partners += [(lon, lat, mem_o)]
     partners += [
         (lon_w, lat, mem), (lon_e, lat, mem),
         (lon_w, lat_n, mem), (lon_w, lat_s, mem), (lon_e, lat_n, mem), (lon_e, lat_s, mem),
     ]
     for where in partners:
         pl.semaphore_signal(barrier, inc=1, device_id=where, device_id_type=MESH)
-    for load in loads:
-        load.wait()
-    live = band_ref[0, 1] - band_ref[0, 0]
-    last[...] = tok[:, pl.ds(jnp.clip(live - 1, 0, SLOTS - 1) + shift, 1)].reshape(MEMBERS, COLS, LEVELS, C)
+    loads[0].wait()
+    loads[1].wait()
     pl.semaphore_wait(barrier, len(partners))
 
     def copy(src, dst, ssem, rsem, where):
@@ -76,12 +89,16 @@
         )
 
     firsts = []
-    for d in range(2):
-        for what, (src, got) in enumerate(((own_d, got_d), (own_u, got_u))):
-            lat_t = 2 * ((2 * d + what + 2 * (xx // 2)) % 4) + yh
-            i = 4 * d + 2 * what
-            firsts.append((lat_t != lat, copy(src, got.at[lat], s1_send.at[i], s1_recv.at[lat], (lon, lat_t, mem))))
-            firsts.append((None, copy(src, got.at[lat], s1_send.at[i + 1], s1_recv.at[lat], (lon_o, lat_t, mem_o))))
+
+    def first(src, dst, i, slot, k, kind):
+        lat_t = 2 * ((k + 2 * mem * MIX) % 4) + kind
+        lat_f = 2 * ((k + 2 * mem_o * MIX) % 4) + kind
+        firsts.append((lat_t != lat, copy(src, dst, s1_send.at[i], s1_recv.at[slot], (lon, lat_t, mem))))
+        firsts.append((None, copy(src, dst, s1_send.at[i + 1], s1_recv.at[slot], (lon_o, lat_f, mem_o))))
+
+    first(own_d, got_d.at[lat % 4], 0, lat % 4, yh + 2 * (lat // 4), 0)
+    for h in range(2):
+        first(own_u.at[:, 384 * h : 384 * (h + 1)], got_u.at[lat], 2 + 2 * h, lat, yh + 2 * h, 1)
 
     def each(op):
         for when, cp in firsts:
@@ -94,6 +111,39 @@
 
     each(lambda cp: cp.start())
 
+    for load in loads[2:]:
+        load.wait()
+    live = band_ref[0, 1] - band_ref[0, 0]
+    last[...] = tok[:, pl.ds(jnp.clip(live - 1, 0, SLOTS - 1) + shift, 1)].reshape(MEMBERS, COLS, LEVELS, C)
+    halves = tok.reshape(MEMBERS, HALF, 2, COLS, LEVELS, C)
+    for m in range(MEMBERS):
+        for i, box in ((0, first_col), (COLS - 1, last_col)):
+            a, b = halves[m, :, 0, i], halves[m, :, 1, i]
+            box[m, :, 0] = a[:, :, :128]
+            box[m, :, 1] = b[:, :, :128]
+            box[m, :, 2] = jnp.concatenate([a[:, :, 128:], b[:, :, 128:]], axis=2)
+
+    cols = [
+        [
+            copy(first_col.at[m], east.at[m], col_send.at[m, 0], col_recv.at[m, 0], (lon_w, lat, mem)),
+            copy(last_col.at[m], west.at[m], col_send.at[m, 1], col_recv.at[m, 1], (lon_e, lat, mem)),
+        ]
+        for m in range(MEMBERS)
+    ]
+    def start_cols(far):
+        for m in range(MEMBERS):
+            @pl.when(yh == far)
+            def _():
+                cols[m][1].start()
+
+            @pl.when(yh != far)
+            def _():
+                cols[m][0].start()
+
+    for far in range(2):
+        if COLS_AT[far] == -2:
+            start_cols(far)
+
     to_next = [
         copy(last, north.at[:, 1 : COLS + 1], row_send.at[0], row_recv.at[0], (lon, lat_s, mem)),
         copy(last.at[:, 0], north.at[:, COLS + 1], row_send.at[1], row_recv.at[1], (lon_w, lat_s, mem)),
@@ -123,25 +173,21 @@
     def _():
         north[...] = jnp.zeros_like(north)
 
-    cols = [
-        copy(tok.at[:, pl.ds(shift, SLOTS), 0], east.at[:, pl.ds(shift, SLOTS)], col_send.at[0], col_recv.at[0], (lon_w, lat, mem)),
-        copy(tok.at[:, pl.ds(shift, SLOTS), COLS - 1], west.at[:, pl.ds(shift, SLOTS)], col_send.at[1], col_recv.at[1], (lon_e, lat, mem)),
-    ]
-
     spot = (live + shift) // 2
     gains, shifts = dg[...].reshape(1, 4 * C), ds[...].reshape(1, 4 * C)
 
     def cell(m, j, q, p):
         i = 2 * j + q
-        if i == 0:
-            x = west.reshape(MEMBERS, HALF, 2, LEVELS, C)[m, :, p]
-        elif i == COLS + 1:
-            x = east.reshape(MEMBERS, HALF, 2, LEVELS, C)[m, :, p]
+        where = lax.broadcasted_iota(jnp.int32, (HALF, LEVELS, C), 0)
+        if i in (0, COLS + 1):
+            box = east if i else west
+            x = jnp.concatenate([box[m, :, p], box[m, :, 2][:, :, 64 * p : 64 * p + 64]], axis=2)
+            if p == 0:
+                x = jnp.where(where + 1 == shift, north[m, i].reshape(1, LEVELS, C), x)
         else:
             x = tok.reshape(MEMBERS, HALF, 2, COLS, LEVELS, C)[m, :, p, i - 1]
         if p:
-            here = lax.broadcasted_iota(jnp.int32, (HALF, LEVELS, C), 0) == spot
-            x = jnp.where(here, south[m, i].reshape(1, LEVELS, C), x)
+            x = jnp.where(where == spot, south[m, i].reshape(1, LEVELS, C), x)
         return x.reshape(HALF * LEVELS, C).astype(F32)
 
     def norm(j):
@@ -174,99 +220,104 @@
         norm(2)
 
     def border():
-        for cp in cols:
+        for cp in cols[0] + cols[1]:
             cp.wait_recv()
-
-        @pl.when(lat > 0)
-        def _():
-            west[:, 0] = north[:, 0]
-            east[:, 0] = north[:, COLS + 1]
-
         norm(0)
         norm(3)
 
-    def gather(own, got, flat, full, rows, other, rows_o):
-        span, span_o = 8 * rows, 8 * rows_o
-        home = yh == core
+    def gather(home, parts, keep, got, flat, rows, full, mine):
+        count = 24 // rows
 
         @pl.when(home)
         def _():
-            got[pl.ds(lat, 1)] = own[...].reshape(1, *own.shape)
-
-        for i in range(8):
-            @pl.when(jnp.logical_not(jnp.logical_and(home, lat == i)))
+            keep()
+
+        for i in range(count):
+            @pl.when(jnp.logical_not(jnp.logical_and(home, lat % count == i)))
             def _():
-                copy(own, got.at[i], s1_send.at[0], s1_recv.at[i], mate).wait_recv()
-
-        for i in range(8):
+                copy(parts, got.at[i], s1_send.at[0], s1_recv.at[i], mate).wait_recv()
+
+        for i in range(count):
             flat[rows * i : rows * (i + 1), :] = got[i].astype(F32)
-
-        def mine(b):
-            return full.at[b, pl.ds(pl.multiple_of(core * span, 8), span)]
-
-        def theirs(b):
-            return full.at[b, pl.ds(pl.multiple_of((1 - core) * span, 8), span)]
-
-        def cross(b):
-            return other.at[b, pl.ds(pl.multiple_of(core * span_o, 8), span_o)]
-
-        def cross_theirs(b):
-            return other.at[b, pl.ds(pl.multiple_of((1 - core) * span_o, 8), span_o)]
-
-        full[pl.ds(z, 1), pl.ds(pl.multiple_of(core * span, 8), span), :] = flat[...].astype(BF).reshape(1, *flat.shape)
-        order = (0,) + ORDER
+        mine(z)[...] = flat[...].astype(BF).reshape(1, 24, 384)
         z_out = [copy(mine(z), mine(z), z_send.at[d], z_recv.at[d], along(d)) for d in ORDER]
         for cp in z_out:
             cp.start()
-        for cp in cols:
-            cp.start()
+        for far in range(2):
+            if COLS_AT[far] == -1:
+                start_cols(far)
         started = []
 
-        def pass_on(d):
-            b = (z + NZ - d) % NZ
-            if d:
-                copy(mine(b), mine(b), z_send.at[d], z_recv.at[d], mate).wait_recv()
-            for cp in (
-                copy(mine(b), mine(b), x_send.at[d], x_recv.at[d], beside),
-                copy(mine(b), mine(b), pair_send.at[0, d], pair_recv.at[0, d], mate),
-            ):
+        def pass_on(b, t):
+            part = mine(b)
+            for s in range(2):
+                cp = copy(part, part, x_send.at[s, t], x_recv.at[s, t], across(1 + 2 * s))
                 cp.start()
                 started.append(cp)
-
-        def hand_over(d):
-            b = (z + NZ - d) % NZ
-            copy(cross(b), cross(b), x_send.at[d], x_recv.at[d], beside).wait_recv()
-            cp = copy(cross(b), cross(b), pair_send.at[1, d], pair_recv.at[1, d], mate)
+            side = b % 2
+            cp = copy(part, part, x_send.at[2, t], x_recv.at[2, t], (lon + side * (lon_o - lon), lat, mem_o) if MIX else across(2))
             cp.start()
             started.append(cp)
 
-        arrivals = (0,) + ARRIVE
-        for i, d in enumerate(arrivals):
-            pass_on(d)
-            if i == INSIDE:
+        def hand_over(b, t):
+            part = mine(b)
+            for s in range(3):
+                copy(part, part, x_send.at[s, t], x_recv.at[s, t], mate).wait_recv()
+            whole = full.at[b]
+            cp = copy(whole, whole, pair_send.at[t], pair_recv.at[t], mate)
+            cp.start()
+            started.append(cp)
+
+        blocks = [(z + NZ - d) % NZ for d in (0,) + ARRIVE]
+        for t, d in enumerate((0,) + ARRIVE):
+            if d:
+                copy(mine(z), mine(z), z_send.at[d], z_recv.at[d], mate).wait_recv()
+            pass_on(blocks[t], t)
+            for far in range(2):
+                if COLS_AT[far] == t:
+                    start_cols(far)
+            if t == INSIDE:
                 inside()
-            if i >= LAG:
-                hand_over(arrivals[i - LAG])
-        for d in arrivals[NZ - LAG :]:
-            hand_over(d)
+            if t >= LAG:
+                hand_over(blocks[t - LAG], t - LAG)
+        for t in range(NZ - LAG, NZ):
+            hand_over(blocks[t], t)
         border()
-        for d in arrivals:
-            b = (z + NZ - d) % NZ
-            copy(theirs(b), theirs(b), pair_send.at[0, d], pair_recv.at[0, d], mate).wait_recv()
-            copy(cross_theirs(b), cross_theirs(b), pair_send.at[1, d], pair_recv.at[1, d], mate).wait_recv()
-        for cp in z_out + started:
+        return z_out + started
+
+    def take(other):
+        for t, d in enumerate((0,) + ARRIVE):
+            whole = other.at[(z + NZ - d) % NZ]
+            copy(whole, whole, pair_send.at[t], pair_recv.at[t], mate).wait_recv()
+
+    @pl.when(core == 0)
+    def _():
+        def keep():
+            got_d[pl.ds(lat % 4, 1)] = own_d[...].reshape(1, 6, 384)
+
+        def mine(b, n=1):
+            return wd.at[pl.ds(b, n), pl.ds(pl.multiple_of(48 * cy + 24 * ch, 8), 24)]
+
+        sent = gather(jnp.logical_and(yh == cy, lat // 4 == ch), own_d, keep, got_d, flat, 6, wd, mine)
+        take(wu)
+        for cp in sent:
             cp.wait_send()
 
-    @pl.when(kind == 0)
-    def _():
-        gather(own_d, got_d, flat_d, wd, 6, wu, 3)
-
-    @pl.when(kind == 1)
-    def _():
-        gather(own_u, got_u, flat_u, wu, 3, wd, 6)
+    @pl.when(core == 1)
+    def _():
+        def keep():
+            got_u[pl.ds(lat, 1)] = own_u[:, pl.ds(pl.multiple_of(384 * ch, 128), 384)].reshape(1, 3, 384)
+
+        def mine(b, n=1):
+            return wu.at[pl.ds(b, n), pl.ds(pl.multiple_of(24 * cy, 8), 24), pl.ds(pl.multiple_of(384 * ch, 128), 384)]
+
+        sent = gather(yh == cy, own_u.at[:, :384], keep, got_u, flat, 3, wu, mine)
+        take(wd)
+        for cp in sent:
+            cp.wait_send()
 
     each(lambda cp: cp.wait_send())
-    for cp in cols:
+    for cp in cols[0] + cols[1]:
         cp.wait_send()
 
     @pl.when(lat < 7)
@@ -284,7 +335,7 @@
     dma = pltpu.SemaphoreType.DMA
     vmem = pl.BlockSpec(memory_space=pltpu.VMEM)
     hbm = pl.BlockSpec(memory_space=pltpu.HBM)
-    col = (MEMBERS, EXT, LEVELS, C)
+    col = (MEMBERS, HALF, 3, LEVELS, 128)
     row = (MEMBERS, COLS + 2, LEVELS, C)
     return pl.pallas_call(
         exchange,
@@ -302,17 +353,18 @@
             pltpu.VMEM((MEMBERS, EXT, COLS, LEVELS, C), BF),
             pltpu.VMEM(col, BF),
             pltpu.VMEM(col, BF),
+            pltpu.VMEM(col, BF),
+            pltpu.VMEM(col, BF),
             pltpu.VMEM(row, BF),
             pltpu.VMEM(row, BF),
             pltpu.VMEM((MEMBERS, COLS, LEVELS, C), BF),
             pltpu.VMEM((6, 384), BF),
             pltpu.VMEM((3, 768), BF),
-            pltpu.VMEM((8, 6, 384), BF),
-            pltpu.VMEM((8, 3, 768), BF),
-            pltpu.VMEM((48, 384), F32),
-            pltpu.VMEM((24, 768), F32),
-            dma((6,)), dma((8,)), dma((8,)), dma((NZ,)), dma((NZ,)), dma((NZ,)), dma((NZ,)),
-            dma((2, NZ)), dma((2, NZ)), dma((2,)), dma((2,)), dma((6,)), dma((6,)),
+            pltpu.VMEM((4, 6, 384), BF),
+            pltpu.VMEM((8, 3, 384), BF),
+            pltpu.VMEM((24, 384), F32),
+            dma((6,)), dma((8,)), dma((8,)), dma((NZ,)), dma((NZ,)), dma((3, NZ)), dma((3, NZ)),
+            dma((NZ,)), dma((NZ,)), dma((2, 2)), dma((2, 2)), dma((6,)), dma((6,)),
         ],
         compiler_params=pltpu.CompilerParams(
             collective_id=0, has_side_effects=True, vmem_limit_bytes=24 << 20

time: 38.8 us -> 36.9 us (0.951)
  Pallas kernels: 38.7 us -> 36.7 us
    pallas_call x1, Pallas kernels: 31.8 us -> 29.9 us  [run_exchange(): pl.pallas_call(exchange, out_shape=[jax.ShapeDtypeStruct((NZ, 96, 384), B...]
where the time goes in v5:
time: 36.9 us; the launch traced here: 36.8 us
  Pallas kernels  36.7 us (99%)
    pallas_call x1, Pallas kernels, run_exchange(): pl.pallas_call(exchange, out_shape=[jax.ShapeDtypeStruct((NZ, 96, 384), B...  29.9 us
    pallas_call x1, Pallas kernels, run_patches(): pl.pallas_call(patches, out_shape=jax.ShapeDtypeStruct((MEMBERS, SLOTS, C...  6.88 us

profile of v5, /device:TPU:1, one launch (start us, length us, event | category | flops | bytes accessed | tf_op | source)
XLA Modules:
  0.0 36.8 jit_solution(1880641887109202501)
XLA Ops:
  0.0 0.0 copy-start.1
  0.0 0.0 copy-start
  0.0 29.9 %exchange.1 = (bf16[8,96,384]{2,1,0:T(8,128)(2,1)S(1)}, bf16[8,48,768]{2,1,0:T(8,128)(2,1)S(1)}, bf16[4,4,2,144,192]{4,3,2,1,0:T(8,128)(2,1)S(1)}) custom-call(s32[1,2]{1,0:T(1,128)} %band_hbm.3, bf16[2,34,6,8,192]{4,3,2,1,0:T(8,128)(2,1)} %bitcast.6, bf16[6,384]{1,0:T(8,128)(2,1)} %down_hbm.1, bf16[3,768]{1,0:T(4,128)(2,1)} %up_hbm.1, f32[768]{0:T(1024)} %dg_hbm.1, ...), custom_call_target="tpu_custom_call" | custom-call | tf_op jit(solution)/shard_map/exchange/pallas_call | solution.py:340
  29.9 0.0 copy-done.1
  29.9 0.0 copy-done
  29.9 6.9 %patches.1 = bf16[2,34,6,8,192]{4,3,2,1,0:T(8,128)(2,1)} custom-call(s32[1,2]{1,0:T(1,128)} %band_hbm.3, bf16[768,384]{1,0:T(8,128)(2,1)S(1)} %bitcast.4, bf16[384,768]{1,0:T(8,128)(2,1)S(1)} %bitcast.5, bf16[4,4,2,144,192]{4,3,2,1,0:T(8,128)(2,1)S(1)} %get-tuple-element.10.normed, f32[192]{0:T(256)S(1)} %copy-done, f32[192]{0:T(256)S(1)} %copy-done.1, ...), custom_call_target="tpu_custom_call" | custom-call | tf_op jit(solution)/shard_map/patches/pallas_call | solution.py:438
Async XLA Ops:
  0.0 29.9 %copy-start.1 = (f32[192]{0:T(256)S(1)}, f32[192]{0:T(256)}, u32[]{:S(2)}) copy-start(f32[192]{0:T(256)} %us.1) | copy-start | bytes 2308
  0.0 29.9 %copy-start = (f32[192]{0:T(256)S(1)}, f32[192]{0:T(256)}, u32[]{:S(2)}) copy-start(f32[192]{0:T(256)} %ug.1) | copy-start | bytes 2308

commit v6 on v5

--- a/solution.py
+++ b/solution.py
@@ -199,10 +199,12 @@
             cells = {key: x - average for key, x in cells.items()}
             total = sum(jnp.sum(x * x, axis=1, keepdims=True) for x in cells.values())
             scale = lax.rsqrt(total * (1.0 / (4 * C)) + 1e-05)
+            done = []
             for (q, p), x in cells.items():
                 g = 2 * q + p
                 y = x * scale * gains[:, C * g : C * (g + 1)] + shifts[:, C * g : C * (g + 1)]
-                normed[g, j, m] = y.astype(BF)
+                done.append(y.astype(BF))
+            normed[j, m] = jnp.concatenate(done, axis=1)
 
     def inside():
         @pl.when(lat < 7)
@@ -225,7 +227,11 @@
         norm(0)
         norm(3)
 
-    def gather(home, parts, keep, got, flat, rows, full, mine):
+    def centre(w):
+        blocks = [w[:, :C], w[:, C:]]
+        return jnp.concatenate([v - jnp.sum(v, axis=1, keepdims=True) * (1.0 / C) for v in blocks], axis=1)
+
+    def gather(home, finish, parts, keep, got, flat, rows, full, mine):
         count = 24 // rows
 
         @pl.when(home)
@@ -239,7 +245,7 @@
 
         for i in range(count):
             flat[rows * i : rows * (i + 1), :] = got[i].astype(F32)
-        mine(z)[...] = flat[...].astype(BF).reshape(1, 24, 384)
+        mine(z)[...] = finish(flat[...]).astype(BF).reshape(1, 24, 384)
         z_out = [copy(mine(z), mine(z), z_send.at[d], z_recv.at[d], along(d)) for d in ORDER]
         for cp in z_out:
             cp.start()
@@ -298,7 +304,7 @@
         def mine(b, n=1):
             return wd.at[pl.ds(b, n), pl.ds(pl.multiple_of(48 * cy + 24 * ch, 8), 24)]
 
-        sent = gather(jnp.logical_and(yh == cy, lat // 4 == ch), own_d, keep, got_d, flat, 6, wd, mine)
+        sent = gather(jnp.logical_and(yh == cy, lat // 4 == ch), lambda w: w, own_d, keep, got_d, flat, 6, wd, mine)
         take(wu)
         for cp in sent:
             cp.wait_send()
@@ -311,7 +317,7 @@
         def mine(b, n=1):
             return wu.at[pl.ds(b, n), pl.ds(pl.multiple_of(24 * cy, 8), 24), pl.ds(pl.multiple_of(384 * ch, 128), 384)]
 
-        sent = gather(yh == cy, own_u.at[:, :384], keep, got_u, flat, 3, wu, mine)
+        sent = gather(yh == cy, centre, own_u.at[:, :384], keep, got_u, flat, 3, wu, mine)
         take(wd)
         for cp in sent:
             cp.wait_send()
@@ -342,7 +348,7 @@
         out_shape=[
             jax.ShapeDtypeStruct((NZ, 96, 384), BF),
             jax.ShapeDtypeStruct((NZ, 48, 768), BF),
-            jax.ShapeDtypeStruct((4, 4, MEMBERS, HALF * LEVELS, C), BF),
+            jax.ShapeDtypeStruct((4, MEMBERS, HALF * LEVELS, 4 * C), BF),
         ],
         in_specs=[hbm] * 6,
         out_specs=[vmem] * 3,
@@ -393,17 +399,13 @@
         wu4[g] = wu[:, C * g : C * (g + 1)]
     eps = 1e-05
     fine_gain, fine_shift = ug[...].reshape(1, C), us[...].reshape(1, C)
-    rows_out = fine.reshape(MEMBERS, EXT, COLS, LEVELS, C)
+    pairs = out_hbm.reshape(MEMBERS, SLOTS // 2, 2, COLS, LEVELS, C)
     stores = []
     for members in SPLIT:
-        def pick(g):
-            return jnp.concatenate([normed[g, j, m] for j in range(4) for m in members], axis=0)
-
-        coarse = None
-        for g in range(4):
-            term = jnp.dot(pick(g), wd[C * g : C * (g + 1), :], preferred_element_type=F32)
-            coarse = term if coarse is None else coarse + term
-        coarse = coarse.astype(BF)
+        def pick():
+            return jnp.concatenate([normed[j, m] for j in range(4) for m in members], axis=0)
+
+        coarse = jnp.dot(pick(), wd[...], preferred_element_type=F32).astype(BF)
         if members == SPLIT[0]:
             for load in loads:
                 load.wait()
@@ -414,8 +416,6 @@
             for q in range(2):
                 j0 = 1 - q
                 grown = jnp.dot(coarse[n * j0 : n * (j0 + 3)], wu4[2 * p + q], preferred_element_type=F32)
-                average = jnp.sum(grown, axis=1, keepdims=True) * (1.0 / C)
-                grown = grown - average
                 spread = jnp.sum(grown * grown, axis=1, keepdims=True) * (1.0 / C)
                 unit = (grown * lax.rsqrt(spread + eps) * fine_gain + fine_shift).astype(BF)
                 done = jnp.dot(unit, mix[...], preferred_element_type=F32).astype(BF)
@@ -423,10 +423,14 @@
                 for j in range(3):
                     for i, m in enumerate(members):
                         fine[m, :, p, 2 * (j + j0) + q - 1] = jnp.where(keep, done[j, i], jnp.zeros_like(done[j, i]))
-        for m in members:
-            store = pltpu.make_async_copy(rows_out.at[m, pl.ds(shift, SLOTS)], out_hbm.at[m], store_sem.at[m])
-            store.start()
-            stores.append(store)
+            for m in members:
+                store = pltpu.make_async_copy(
+                    fine.at[m, pl.ds(shift * (1 - p), SLOTS // 2), p],
+                    pairs.at[m, :, p + shift - 2 * p * shift],
+                    store_sem.at[m, p],
+                )
+                store.start()
+                stores.append(store)
     for store in stores:
         store.wait()
 
@@ -446,7 +450,7 @@
             pltpu.VMEM((MEMBERS, HALF, 2, COLS, LEVELS, C), BF),
             pltpu.VMEM((4, 2 * C, C), BF),
             pltpu.SemaphoreType.DMA((2,)),
-            pltpu.SemaphoreType.DMA((MEMBERS,)),
+            pltpu.SemaphoreType.DMA((MEMBERS, 2)),
         ],
         compiler_params=pltpu.CompilerParams(vmem_limit_bytes=24 << 20),
         name="patches",

time: 36.9 us -> 35.5 us (0.962)
  Pallas kernels: 36.7 us -> 35.3 us
    pallas_call x1, Pallas kernels: 6.88 us -> 5.39 us  [run_patches(): pl.pallas_call(patches, out_shape=jax.ShapeDtypeStruct((MEMBERS, SLOTS, C...]
where the time goes in v6:
time: 35.5 us; the launch traced here: 35.4 us
  Pallas kernels  35.3 us (99%)
    pallas_call x1, Pallas kernels, run_exchange(): pl.pallas_call(exchange, out_shape=[jax.ShapeDtypeStruct((NZ, 96, 384), B...  29.9 us
    pallas_call x1, Pallas kernels, run_patches(): pl.pallas_call(patches, out_shape=jax.ShapeDtypeStruct((MEMBERS, SLOTS, C...  5.39 us

profile of v6, /device:TPU:1, one launch (start us, length us, event | category | flops | bytes accessed | tf_op | source)
XLA Modules:
  0.0 35.4 jit_solution(12710347235392016755)
XLA Ops:
  0.0 0.0 copy-start.1
  0.0 0.0 copy-start
  0.0 29.9 %exchange.1 = (bf16[8,96,384]{2,1,0:T(8,128)(2,1)S(1)}, bf16[8,48,768]{2,1,0:T(8,128)(2,1)S(1)}, bf16[4,2,144,768]{3,2,1,0:T(8,128)(2,1)S(1)}) custom-call(s32[1,2]{1,0:T(1,128)} %band_hbm.3, bf16[2,34,6,8,192]{4,3,2,1,0:T(8,128)(2,1)} %bitcast.6, bf16[6,384]{1,0:T(8,128)(2,1)} %down_hbm.1, bf16[3,768]{1,0:T(4,128)(2,1)} %up_hbm.1, f32[768]{0:T(1024)} %dg_hbm.1, ...), custom_call_target="tpu_custom_call" | custom-call | tf_op jit(solution)/shard_map/exchange/pallas_call | solution.py:346
  30.0 0.0 copy-done.1
  30.0 0.0 copy-done
  30.0 5.4 %patches.1 = bf16[2,34,6,8,192]{4,3,2,1,0:T(8,128)(2,1)} custom-call(s32[1,2]{1,0:T(1,128)} %band_hbm.3, bf16[768,384]{1,0:T(8,128)(2,1)S(1)} %bitcast.4, bf16[384,768]{1,0:T(8,128)(2,1)S(1)} %bitcast.5, bf16[4,2,144,768]{3,2,1,0:T(8,128)(2,1)S(1)} %get-tuple-element.10.normed, f32[192]{0:T(256)S(1)} %copy-done, f32[192]{0:T(256)S(1)} %copy-done.1, ...), custom_call_target="tpu_custom_call" | custom-call | tf_op jit(solution)/shard_map/patches/pallas_call | solution.py:442
Async XLA Ops:
  0.0 30.0 %copy-start.1 = (f32[192]{0:T(256)S(1)}, f32[192]{0:T(256)}, u32[]{:S(2)}) copy-start(f32[192]{0:T(256)} %us.1) | copy-start | bytes 2308
  0.0 30.0 %copy-start = (f32[192]{0:T(256)S(1)}, f32[192]{0:T(256)}, u32[]{:S(2)}) copy-start(f32[192]{0:T(256)} %ug.1) | copy-start | bytes 2308

commit v7 on v6

--- a/solution.py
+++ b/solution.py
@@ -15,6 +15,7 @@
 ORDER = (1, 7, 2, 6, 3, 5, 4)
 ARRIVE = (1, 7, 2, 6, 3, 5, 4)
 LAG = 6
+BORDER_AT = (7, 8)
 INSIDE = 0
 COLS_AT = (-1, -1)
 MIX = 0
@@ -190,20 +191,24 @@
             x = jnp.where(where == spot, south[m, i].reshape(1, LEVELS, C), x)
         return x.reshape(HALF * LEVELS, C).astype(F32)
 
-    def norm(j):
-        @pl.loop(0, MEMBERS)
-        def _(m):
-            cells = {(q, p): cell(m, j, q, p) for q in range(2) for p in range(2)}
-            total = sum(jnp.sum(x, axis=1, keepdims=True) for x in cells.values())
-            average = total * (1.0 / (4 * C))
-            cells = {key: x - average for key, x in cells.items()}
-            total = sum(jnp.sum(x * x, axis=1, keepdims=True) for x in cells.values())
-            scale = lax.rsqrt(total * (1.0 / (4 * C)) + 1e-05)
+    def norm(js, m):
+        keys = [(j, q, p) for j in js for q in range(2) for p in range(2)]
+        cells = {key: cell(m, *key) for key in keys}
+        average, scale = {}, {}
+        for j in js:
+            total = sum(jnp.sum(cells[key], axis=1, keepdims=True) for key in keys if key[0] == j)
+            average[j] = total * (1.0 / (4 * C))
+        cells = {key: x - average[key[0]] for key, x in cells.items()}
+        for j in js:
+            total = sum(jnp.sum(cells[key] * cells[key], axis=1, keepdims=True) for key in keys if key[0] == j)
+            scale[j] = lax.rsqrt(total * (1.0 / (4 * C)) + 1e-05)
+        for j in js:
             done = []
-            for (q, p), x in cells.items():
-                g = 2 * q + p
-                y = x * scale * gains[:, C * g : C * (g + 1)] + shifts[:, C * g : C * (g + 1)]
-                done.append(y.astype(BF))
+            for q in range(2):
+                for p in range(2):
+                    g = 2 * q + p
+                    y = cells[j, q, p] * scale[j] * gains[:, C * g : C * (g + 1)] + shifts[:, C * g : C * (g + 1)]
+                    done.append(y.astype(BF))
             normed[j, m] = jnp.concatenate(done, axis=1)
 
     def inside():
@@ -218,14 +223,13 @@
                 cp.wait_recv()
             tok[:, 0] = north[:, 1 : COLS + 1]
 
-        norm(1)
-        norm(2)
-
-    def border():
-        for cp in cols[0] + cols[1]:
+        for m in range(MEMBERS):
+            norm((1, 2), m)
+
+    def border(m):
+        for cp in cols[m]:
             cp.wait_recv()
-        norm(0)
-        norm(3)
+        norm((0, COLS // 2), m)
 
     def centre(w):
         blocks = [w[:, :C], w[:, C:]]
@@ -266,6 +270,9 @@
             started.append(cp)
 
         def hand_over(b, t):
+            for m in range(MEMBERS):
+                if t == BORDER_AT[m]:
+                    border(m)
             part = mine(b)
             for s in range(3):
                 copy(part, part, x_send.at[s, t], x_recv.at[s, t], mate).wait_recv()
@@ -288,7 +295,9 @@
                 hand_over(blocks[t - LAG], t - LAG)
         for t in range(NZ - LAG, NZ):
             hand_over(blocks[t], t)
-        border()
+        for m in range(MEMBERS):
+            if BORDER_AT[m] == NZ:
+                border(m)
         return z_out + started
 
     def take(other):

time: 35.5 us -> 34.2 us (0.963)
  Pallas kernels: 35.3 us -> 34.1 us
    pallas_call x1, Pallas kernels: 29.9 us -> 28.7 us  [run_exchange(): pl.pallas_call(exchange, out_shape=[jax.ShapeDtypeStruct((NZ, 96, 384), B...]
where the time goes in v7:
time: 34.2 us; the launch traced here: 34.1 us
  Pallas kernels  34.1 us (100%)
    pallas_call x1, Pallas kernels, run_exchange(): pl.pallas_call(exchange, out_shape=[jax.ShapeDtypeStruct((NZ, 96, 384), B...  28.7 us
    pallas_call x1, Pallas kernels, run_patches(): pl.pallas_call(patches, out_shape=jax.ShapeDtypeStruct((MEMBERS, SLOTS, C...  5.4 us

profile of v7, /device:TPU:1, one launch (start us, length us, event | category | flops | bytes accessed | tf_op | source)
XLA Modules:
  0.0 34.1 jit_solution(10649752344893076741)
XLA Ops:
  0.0 0.0 copy-start.1
  0.0 0.0 copy-start
  0.0 28.7 %exchange.1 = (bf16[8,96,384]{2,1,0:T(8,128)(2,1)S(1)}, bf16[8,48,768]{2,1,0:T(8,128)(2,1)S(1)}, bf16[4,2,144,768]{3,2,1,0:T(8,128)(2,1)S(1)}) custom-call(s32[1,2]{1,0:T(1,128)} %band_hbm.3, bf16[2,34,6,8,192]{4,3,2,1,0:T(8,128)(2,1)} %bitcast.6, bf16[6,384]{1,0:T(8,128)(2,1)} %down_hbm.1, bf16[3,768]{1,0:T(4,128)(2,1)} %up_hbm.1, f32[768]{0:T(1024)} %dg_hbm.1, ...), custom_call_target="tpu_custom_call" | custom-call | tf_op jit(solution)/shard_map/exchange/pallas_call | solution.py:355
  28.7 0.0 copy-done.1
  28.7 0.0 copy-done
  28.7 5.4 %patches.1 = bf16[2,34,6,8,192]{4,3,2,1,0:T(8,128)(2,1)} custom-call(s32[1,2]{1,0:T(1,128)} %band_hbm.3, bf16[768,384]{1,0:T(8,128)(2,1)S(1)} %bitcast.4, bf16[384,768]{1,0:T(8,128)(2,1)S(1)} %bitcast.5, bf16[4,2,144,768]{3,2,1,0:T(8,128)(2,1)S(1)} %get-tuple-element.10.normed, f32[192]{0:T(256)S(1)} %copy-done, f32[192]{0:T(256)S(1)} %copy-done.1, ...), custom_call_target="tpu_custom_call" | custom-call | tf_op jit(solution)/shard_map/patches/pallas_call | solution.py:451
Async XLA Ops:
  0.0 28.7 %copy-start.1 = (f32[192]{0:T(256)S(1)}, f32[192]{0:T(256)}, u32[]{:S(2)}) copy-start(f32[192]{0:T(256)} %us.1) | copy-start | bytes 2308
  0.0 28.7 %copy-start = (f32[192]{0:T(256)S(1)}, f32[192]{0:T(256)}, u32[]{:S(2)}) copy-start(f32[192]{0:T(256)} %ug.1) | copy-start | bytes 2308

commit v8 on v7

--- a/solution.py
+++ b/solution.py
@@ -389,6 +389,8 @@
 
 
 SPLIT = ((0, 1),)
+WIDE = 3
+DEPTH = 1
 ROWS = HALF * LEVELS
 
 
@@ -420,18 +422,22 @@
                 load.wait()
             bound = band_ref[0, 1] - band_ref[0, 0] + shift
         n = ROWS * len(members)
-        for p in range(2):
-            keep = 2 * lax.broadcasted_iota(jnp.int32, (HALF, LEVELS, C), 0) + p < bound
-            for q in range(2):
-                j0 = 1 - q
-                grown = jnp.dot(coarse[n * j0 : n * (j0 + 3)], wu4[2 * p + q], preferred_element_type=F32)
-                spread = jnp.sum(grown * grown, axis=1, keepdims=True) * (1.0 / C)
-                unit = (grown * lax.rsqrt(spread + eps) * fine_gain + fine_shift).astype(BF)
-                done = jnp.dot(unit, mix[...], preferred_element_type=F32).astype(BF)
-                done = done.reshape(3, len(members), HALF, LEVELS, C)
-                for j in range(3):
-                    for i, m in enumerate(members):
-                        fine[m, :, p, 2 * (j + j0) + q - 1] = jnp.where(keep, done[j, i], jnp.zeros_like(done[j, i]))
+        keeps = [2 * lax.broadcasted_iota(jnp.int32, (HALF, LEVELS, C), 0) + p < bound for p in range(2)]
+
+        def expand(p, q, j, w):
+            r = n * (j + 1 - q)
+            return jnp.dot(coarse[r : r + n * w], wu4[2 * p + q], preferred_element_type=F32)
+
+        def settle(grown, p, q, j, w):
+            spread = jnp.sum(grown * grown, axis=1, keepdims=True) * (1.0 / C)
+            unit = (grown * lax.rsqrt(spread + eps) * fine_gain + fine_shift).astype(BF)
+            done = jnp.dot(unit, mix[...], preferred_element_type=F32).astype(BF)
+            done = done.reshape(w, len(members), HALF, LEVELS, C)
+            for k in range(w):
+                for i, m in enumerate(members):
+                    fine[m, :, p, 2 * (j + k) + 1 - q] = jnp.where(keeps[p], done[k, i], jnp.zeros_like(done[k, i]))
+
+        def leave(p):
             for m in members:
                 store = pltpu.make_async_copy(
                     fine.at[m, pl.ds(shift * (1 - p), SLOTS // 2), p],
@@ -440,6 +446,17 @@
                 )
                 store.start()
                 stores.append(store)
+
+        items = [(p, q, j, WIDE) for p in range(2) for q in range(2) for j in range(0, 3, WIDE)]
+        ahead = []
+        for item in items + [None] * DEPTH:
+            if item is not None:
+                ahead.append((item, expand(*item)))
+            if len(ahead) > DEPTH or item is None:
+                old, grown = ahead.pop(0)
+                settle(grown, *old)
+                if old[1] == 1 and old[2] + WIDE == 3:
+                    leave(old[0])
     for store in stores:
         store.wait()
 

time: 34.2 us -> 33.2 us (0.971)
  Pallas kernels: 34.1 us -> 33 us
    pallas_call x1, Pallas kernels: 5.4 us -> 4.35 us  [run_patches(): pl.pallas_call(patches, out_shape=jax.ShapeDtypeStruct((MEMBERS, SLOTS, C...]
where the time goes in v8:
time: 33.2 us; the launch traced here: 33.1 us
  Pallas kernels  33 us (99%)
    pallas_call x1, Pallas kernels, run_exchange(): pl.pallas_call(exchange, out_shape=[jax.ShapeDtypeStruct((NZ, 96, 384), B...  28.7 us
    pallas_call x1, Pallas kernels, run_patches(): pl.pallas_call(patches, out_shape=jax.ShapeDtypeStruct((MEMBERS, SLOTS, C...  4.35 us

profile of v8, /device:TPU:1, one launch (start us, length us, event | category | flops | bytes accessed | tf_op | source)
XLA Modules:
  0.0 33.1 jit_solution(3608136751192670844)
XLA Ops:
  0.0 0.0 copy-start.1
  0.0 0.0 copy-start
  0.0 28.7 %exchange.1 = (bf16[8,96,384]{2,1,0:T(8,128)(2,1)S(1)}, bf16[8,48,768]{2,1,0:T(8,128)(2,1)S(1)}, bf16[4,2,144,768]{3,2,1,0:T(8,128)(2,1)S(1)}) custom-call(s32[1,2]{1,0:T(1,128)} %band_hbm.3, bf16[2,34,6,8,192]{4,3,2,1,0:T(8,128)(2,1)} %bitcast.6, bf16[6,384]{1,0:T(8,128)(2,1)} %down_hbm.1, bf16[3,768]{1,0:T(4,128)(2,1)} %up_hbm.1, f32[768]{0:T(1024)} %dg_hbm.1, ...), custom_call_target="tpu_custom_call" | custom-call | tf_op jit(solution)/shard_map/exchange/pallas_call | solution.py:355
  28.7 0.0 copy-done.1
  28.7 0.0 copy-done
  28.7 4.3 %patches.1 = bf16[2,34,6,8,192]{4,3,2,1,0:T(8,128)(2,1)} custom-call(s32[1,2]{1,0:T(1,128)} %band_hbm.3, bf16[768,384]{1,0:T(8,128)(2,1)S(1)} %bitcast.4, bf16[384,768]{1,0:T(8,128)(2,1)S(1)} %bitcast.5, bf16[4,2,144,768]{3,2,1,0:T(8,128)(2,1)S(1)} %get-tuple-element.10.normed, f32[192]{0:T(256)S(1)} %copy-done, f32[192]{0:T(256)S(1)} %copy-done.1, ...), custom_call_target="tpu_custom_call" | custom-call | tf_op jit(solution)/shard_map/patches/pallas_call | solution.py:468
Async XLA Ops:
  0.0 28.7 %copy-start.1 = (f32[192]{0:T(256)S(1)}, f32[192]{0:T(256)}, u32[]{:S(2)}) copy-start(f32[192]{0:T(256)} %us.1) | copy-start | bytes 2308
  0.0 28.7 %copy-start = (f32[192]{0:T(256)S(1)}, f32[192]{0:T(256)}, u32[]{:S(2)}) copy-start(f32[192]{0:T(256)} %ug.1) | copy-start | bytes 2308

commit v9 on v8

--- a/solution.py
+++ b/solution.py
@@ -396,7 +396,7 @@
 
 def patches(
     band_hbm, wd, wu, normed, ug, us, mix_hbm,
-    out_hbm, band_ref, mix, fine, wu4, load_sem, store_sem,
+    out_hbm, band_ref, mix, fine, load_sem, store_sem,
 ):
     lat = lax.axis_index("lat")
     shift = jnp.minimum(lat, 1)
@@ -406,8 +406,6 @@
     ]
     for load in loads:
         load.start()
-    for g in range(4):
-        wu4[g] = wu[:, C * g : C * (g + 1)]
     eps = 1e-05
     fine_gain, fine_shift = ug[...].reshape(1, C), us[...].reshape(1, C)
     pairs = out_hbm.reshape(MEMBERS, SLOTS // 2, 2, COLS, LEVELS, C)
@@ -426,7 +424,7 @@
 
         def expand(p, q, j, w):
             r = n * (j + 1 - q)
-            return jnp.dot(coarse[r : r + n * w], wu4[2 * p + q], preferred_element_type=F32)
+            return jnp.dot(coarse[r : r + n * w], wu[:, C * (2 * p + q) : C * (2 * p + q + 1)], preferred_element_type=F32)
 
         def settle(grown, p, q, j, w):
             spread = jnp.sum(grown * grown, axis=1, keepdims=True) * (1.0 / C)
@@ -474,7 +472,6 @@
             pltpu.SMEM((1, 2), jnp.int32),
             pltpu.VMEM((C, C), BF),
             pltpu.VMEM((MEMBERS, HALF, 2, COLS, LEVELS, C), BF),
-            pltpu.VMEM((4, 2 * C, C), BF),
             pltpu.SemaphoreType.DMA((2,)),
             pltpu.SemaphoreType.DMA((MEMBERS, 2)),
         ],

time: 33.2 us -> 32.6 us (0.982)
  Pallas kernels: 33 us -> 32.5 us
    pallas_call x1, Pallas kernels: 4.35 us -> 3.82 us  [run_patches(): pl.pallas_call(patches, out_shape=jax.ShapeDtypeStruct((MEMBERS, SLOTS, C...]
where the time goes in v9:
time: 32.6 us; the launch traced here: 32.5 us
  Pallas kernels  32.5 us (100%)
    pallas_call x1, Pallas kernels, run_exchange(): pl.pallas_call(exchange, out_shape=[jax.ShapeDtypeStruct((NZ, 96, 384), B...  28.7 us
    pallas_call x1, Pallas kernels, run_patches(): pl.pallas_call(patches, out_shape=jax.ShapeDtypeStruct((MEMBERS, SLOTS, C...  3.82 us

profile of v9, /device:TPU:1, one launch (start us, length us, event | category | flops | bytes accessed | tf_op | source)
XLA Modules:
  0.0 32.5 jit_solution(13251611077849871147)
XLA Ops:
  0.0 0.0 copy-start.1
  0.0 0.0 copy-start
  0.0 28.7 %exchange.1 = (bf16[8,96,384]{2,1,0:T(8,128)(2,1)S(1)}, bf16[8,48,768]{2,1,0:T(8,128)(2,1)S(1)}, bf16[4,2,144,768]{3,2,1,0:T(8,128)(2,1)S(1)}) custom-call(s32[1,2]{1,0:T(1,128)} %band_hbm.3, bf16[2,34,6,8,192]{4,3,2,1,0:T(8,128)(2,1)} %bitcast.6, bf16[6,384]{1,0:T(8,128)(2,1)} %down_hbm.1, bf16[3,768]{1,0:T(4,128)(2,1)} %up_hbm.1, f32[768]{0:T(1024)} %dg_hbm.1, ...), custom_call_target="tpu_custom_call" | custom-call | tf_op jit(solution)/shard_map/exchange/pallas_call | solution.py:355
  28.7 0.0 copy-done.1
  28.7 0.0 copy-done
  28.7 3.8 %patches.1 = bf16[2,34,6,8,192]{4,3,2,1,0:T(8,128)(2,1)} custom-call(s32[1,2]{1,0:T(1,128)} %band_hbm.3, bf16[768,384]{1,0:T(8,128)(2,1)S(1)} %bitcast.4, bf16[384,768]{1,0:T(8,128)(2,1)S(1)} %bitcast.5, bf16[4,2,144,768]{3,2,1,0:T(8,128)(2,1)S(1)} %get-tuple-element.10.normed, f32[192]{0:T(256)S(1)} %copy-done, f32[192]{0:T(256)S(1)} %copy-done.1, ...), custom_call_target="tpu_custom_call" | custom-call | tf_op jit(solution)/shard_map/patches/pallas_call | solution.py:466
Async XLA Ops:
  0.0 28.7 %copy-start.1 = (f32[192]{0:T(256)S(1)}, f32[192]{0:T(256)}, u32[]{:S(2)}) copy-start(f32[192]{0:T(256)} %us.1) | copy-start | bytes 2308
  0.0 28.7 %copy-start = (f32[192]{0:T(256)S(1)}, f32[192]{0:T(256)}, u32[]{:S(2)}) copy-start(f32[192]{0:T(256)} %ug.1) | copy-start | bytes 2308
